TPU v7x, 32 devices: a whole 2x2x4 slice. The times are simulated.
32 devices in a mesh: rep: 4 (over x, y), dp: 8 (over z, core).
Axes of the slice: x: 2, y: 2, z: 4, core: 2. Of those that a mesh axis runs over, the one named last changes fastest.
Arguments:
- g_w_gate: bfloat16 [32, 2, 1024, 3200], P(('rep', 'dp')), parts along dimension 0
- g_w_up: bfloat16 [32, 2, 1024, 3200], P(('rep', 'dp')), parts along dimension 0
- g_w_down: bfloat16 [32, 2, 3200, 1024], P(('rep', 'dp')), parts along dimension 0
- w_gate: bfloat16 [2, 1024, 3200], replicated
- w_up: bfloat16 [2, 1024, 3200], replicated
- w_down: bfloat16 [2, 3200, 1024], replicated
- m_w_gate: float32 [2, 1024, 3200], P(None, 'dp')
- m_w_up: float32 [2, 1024, 3200], P(None, 'dp')
- m_w_down: float32 [2, 3200, 1024], P(None, 'dp')
- v_w_gate: float32 [2, 1024, 3200], P(None, 'dp')
- v_w_up: float32 [2, 1024, 3200], P(None, 'dp')
- v_w_down: float32 [2, 3200, 1024], P(None, 'dp')
Outputs:
- output 1: bfloat16 [8, 1024, 3200], P('rep'), parts along dimension 0
- output 2: bfloat16 [8, 1024, 3200], P('rep'), parts along dimension 0
- output 3: bfloat16 [8, 3200, 1024], P('rep'), parts along dimension 0
- output 4: float32 [8, 1024, 3200], P('rep', 'dp'), parts along dimension 0
- output 5: float32 [8, 1024, 3200], P('rep', 'dp'), parts along dimension 0
- output 6: float32 [8, 3200, 1024], P('rep', 'dp'), parts along dimension 0
- output 7: float32 [8, 1024, 3200], P('rep', 'dp'), parts along dimension 0
- output 8: float32 [8, 1024, 3200], P('rep', 'dp'), parts along dimension 0
- output 9: float32 [8, 3200, 1024], P('rep', 'dp'), parts along dimension 0
There are 4 independent parts. A program takes and returns all parts, laid end to end along the dimension named above; an argument that names none is the same for every part.
All inputs are finite; a program needn't handle non-finite values.
Results may differ from a plain program's by a relative error of at most 0.022.
Values are sent between devices in bfloat16 or wider.
A program may use at most 2 GiB of HBM per device.

v0:
```python
import jax
import jax.numpy as jnp
from jax import lax
from jax.sharding import PartitionSpec as P


def adamw(w, m, v, g):
    m = 0.9 * m + 0.1 * g
    v = 0.95 * v + 0.05 * g * g
    step = m * lax.rsqrt(v + 1e-8) + 0.1 * w
    return (w - 0.02 * step).astype(jnp.bfloat16), m, v


def clipped(gradients, sum_of_squares, count):
    factor = jnp.minimum(1.0, 0.5 * lax.rsqrt(sum_of_squares / count + 1e-30))
    return [g * factor for g in gradients]


def solution(mesh):
    def step(*arrays):
        terms, weights, m, v = (arrays[i : i + 3] for i in (0, 3, 6, 9))
        gradients = [lax.psum_scatter(t[0], "dp", scatter_dimension=1, tiled=True).astype(jnp.float32) for t in terms]
        squares = lax.psum(sum(jnp.sum(g * g) for g in gradients), "dp")
        gradients = clipped(gradients, squares, lax.psum(1, "dp") * sum(g.size for g in gradients))
        me = lax.axis_index("dp")
        own = [lax.dynamic_slice_in_dim(w, me * one.shape[1], one.shape[1], 1).astype(jnp.float32) for w, one in zip(weights, m, strict=True)]
        new = [adamw(w, m, v, g) for w, m, v, g in zip(own, m, v, gradients, strict=True)]
        whole = [lax.all_gather(one[0], "dp", axis=1, tiled=True) for one in new]
        return (*whole, *(one[1] for one in new), *(one[2] for one in new))

    all_of, cut = P(None, None, None), P(None, "dp", None)
    return jax.shard_map(
        step,
        mesh=mesh,
        in_specs=(P(("rep", "dp"), None, None, None),) * 3 + (all_of,) * 3 + (cut,) * 6,
        out_specs=(P("rep", None, None),) * 3 + (P("rep", "dp", None),) * 6,
        check_vma=False,
    )
```

profile of v0, /device:TPU:0, one launch (start us, length us, event | category | flops | bytes accessed | tf_op | source)
XLA Modules:
  0.0 837.6 jit_solution(10890013404015954058)
XLA Ops:
  7.2 0.0 reduce-scatter.4.cloned.1.call-start
  7.2 0.7 reduce-scatter.4.cloned.1.call-update
  7.9 0.0 reduce-scatter.6.cloned.1.call-start
  8.0 0.7 reduce-scatter.6.cloned.1.call-update
  8.7 0.0 reduce-scatter.8.cloned.1.call-start
  8.7 0.7 reduce-scatter.8.cloned.1.call-update
  9.4 0.0 all-gather.8.cloned.1.call-start
  9.4 137.5 %reduce-scatter.4.cloned.1.call-done = bf16[2,128,3200]{2,1,0:T(8,128)(2,1)} async-done(((bf16[2,1024,3200]{2,1,0:T(8,128)(2,1)}), bf16[2,128,3200]{2,1,0:T(8,128)(2,1)}) %reduce-scatter.4.cloned.1.call-update) | async-done | bytes 1638416 | tf_op jit(solution)/shard_map/reduce_scatter | solution.py:22
  147.0 2.9 fusion.9
  149.8 132.1 %reduce-scatter.6.cloned.1.call-done = bf16[2,128,3200]{2,1,0:T(8,128)(2,1)} async-done(((bf16[2,1024,3200]{2,1,0:T(8,128)(2,1)}), bf16[2,128,3200]{2,1,0:T(8,128)(2,1)}) %reduce-scatter.6.cloned.1.call-update) | async-done | bytes 1638416 | tf_op jit(solution)/shard_map/reduce_scatter | solution.py:22
  281.9 2.9 fusion.10
  286.1 130.8 %reduce-scatter.8.cloned.1.call-done = bf16[2,400,1024]{2,1,0:T(8,128)(2,1)} async-done(((bf16[2,3200,1024]{2,1,0:T(8,128)(2,1)}), bf16[2,400,1024]{2,1,0:T(8,128)(2,1)}) %reduce-scatter.8.cloned.1.call-update) | async-done | bytes 1638416 | tf_op jit(solution)/shard_map/reduce_scatter | solution.py:22
  416.9 2.9 fusion.11
  420.4 14.3 %psum.7 = f32[]{:T(128)} all-reduce(f32[]{:T(128)S(6)} %add.65), channel_id=1, replica_groups=mesh['rep'=4,'dp'=8] {'dp'}, use_global_device_ids=true, to_apply=%region_6.0 | all-reduce | flops 1 | bytes 8 | tf_op jit(solution)/shard_map/psum | solution.py:23
  435.4 0.0 copy-start.2
  435.4 6.5 fusion.17
  442.0 0.0 all-gather.8.cloned.1.call-update
  442.0 0.0 all-gather.4.cloned.1.call-start
  442.0 0.0 copy-done.2
  442.0 0.0 copy-start.1
  442.1 6.0 fusion.8
  448.1 0.0 all-gather.4.cloned.1.call-update
  448.1 0.0 all-gather.6.cloned.1.call-start
  448.1 0.0 copy-done.1
  448.1 5.9 fusion.14
  454.0 0.0 all-gather.6.cloned.1.call-update
  454.1 107.0 %all-gather.8.cloned.1.call-done = bf16[2,3200,1024]{2,1,0:T(8,128)(2,1)} async-done(((bf16[2,400,1024]{2,1,0:T(8,128)(2,1)}), bf16[2,3200,1024]{2,1,0:T(8,128)(2,1)}) %all-gather.8.cloned.1.call-update) | async-done | bytes 13107216 | tf_op jit(solution)/shard_map/all_gather | solution.py:28
  561.1 121.4 %all-gather.4.cloned.1.call-done = bf16[2,1024,3200]{2,1,0:T(8,128)(2,1)} async-done(((bf16[2,128,3200]{2,1,0:T(8,128)(2,1)}), bf16[2,1024,3200]{2,1,0:T(8,128)(2,1)}) %all-gather.4.cloned.1.call-update) | async-done | bytes 13107216 | tf_op jit(solution)/shard_map/all_gather | solution.py:28
  682.5 121.5 %all-gather.6.cloned.1.call-done = bf16[2,1024,3200]{2,1,0:T(8,128)(2,1)} async-done(((bf16[2,128,3200]{2,1,0:T(8,128)(2,1)}), bf16[2,1024,3200]{2,1,0:T(8,128)(2,1)}) %all-gather.6.cloned.1.call-update) | async-done | bytes 13107216 | tf_op jit(solution)/shard_map/all_gather | solution.py:28
  804.0 0.0 copy-start
  804.0 0.0 slice-start
  804.0 0.0 slice-start.1
  804.0 0.0 slice-start.2
  804.0 12.7 %copy.24 = bf16[2,1024,3200]{2,1,0:T(8,128)(2,1)} copy(bf16[2,1024,3200]{2,1,0:T(8,128)(2,1)} %all-gather.4.cloned.1.call-done) | data formatting | bytes 26214400
  816.7 0.0 copy-done
  816.7 0.0 slice-start.3
  816.7 6.6 copy.25
  823.3 0.0 slice-done
  823.3 1.2 slice-done.1
  824.5 1.2 slice-done.2
  825.7 0.1 slice-done.3
  825.8 4.9 copy.26
  (1 shorter events, 0.0 us)
Async XLA Ops:
  7.2 139.8 %reduce-scatter.4.cloned.1.call-start = ((), (), s32[]{:S(2)}) async-start(), calls=%async_computation.3 | async-start | bytes 14745600 | tf_op jit(solution)/shard_map/reduce_scatter | solution.py:22
  7.9 274.0 %reduce-scatter.6.cloned.1.call-start = ((), (), s32[]{:S(2)}) async-start(), calls=%async_computation.4 | async-start | bytes 14745600 | tf_op jit(solution)/shard_map/reduce_scatter | solution.py:22
  8.7 408.2 %reduce-scatter.8.cloned.1.call-start = ((), (), s32[]{:S(2)}) async-start(), calls=%async_computation.5 | async-start | bytes 14745600 | tf_op jit(solution)/shard_map/reduce_scatter | solution.py:22
  9.4 551.7 %all-gather.8.cloned.1.call-start = ((), (), s32[]{:S(2)}) async-start(), calls=%async_computation.8 | async-start | bytes 14745600 | tf_op jit(solution)/shard_map/all_gather | solution.py:28
  435.4 6.6 copy-start.2
  442.0 240.5 %all-gather.4.cloned.1.call-start = ((), (), s32[]{:S(2)}) async-start(), calls=%async_computation.6 | async-start | bytes 14745600 | tf_op jit(solution)/shard_map/all_gather | solution.py:28
  442.0 6.1 copy-start.1
  448.1 355.9 %all-gather.6.cloned.1.call-start = ((), (), s32[]{:S(2)}) async-start(), calls=%async_computation.7 | async-start | bytes 14745600 | tf_op jit(solution)/shard_map/all_gather | solution.py:28
  804.0 12.7 %copy-start = (bf16[2,1024,3200]{2,1,0:T(8,128)(2,1)S(1)}, bf16[2,1024,3200]{2,1,0:T(8,128)(2,1)}, u32[]{:S(2)}) copy-start(bf16[2,1024,3200]{2,1,0:T(8,128)(2,1)} %all-gather.6.cloned.1.call-done) | copy-start | bytes 39321604
  804.0 19.4 %slice-start = ((s8[13107200]{0:T(1024)(128)(4,1)}), s8[4194304]{0:T(1024)(128)(4,1)S(1)}, s32[]{:S(2)}) async-start(s8[13107200]{0:T(1024)(128)(4,1)} %bitcast.6), calls=%async_computation.9 | async-start | bytes 8388608
  804.0 20.5 %slice-start.1 = ((s8[13107200]{0:T(1024)(128)(4,1)}), s8[4194304]{0:T(1024)(128)(4,1)S(1)}, s32[]{:S(2)}) async-start(s8[13107200]{0:T(1024)(128)(4,1)} %bitcast.6), calls=%async_computation.10 | async-start | bytes 8388608
  804.0 21.7 %slice-start.2 = ((s8[13107200]{0:T(1024)(128)(4,1)}), s8[4194304]{0:T(1024)(128)(4,1)S(1)}, s32[]{:S(2)}) async-start(s8[13107200]{0:T(1024)(128)(4,1)} %bitcast.6), calls=%async_computation.11 | async-start | bytes 8388608
  816.7 9.1 %slice-start.3 = ((s8[13107200]{0:T(1024)(128)(4,1)}), s8[524288]{0:T(1024)(128)(4,1)S(1)}, s32[]{:S(2)}) async-start(s8[13107200]{0:T(1024)(128)(4,1)} %bitcast.6), calls=%async_computation.12 | async-start | bytes 1048576
Sparse Core Ops, SparseCore 0:
  10.3 136.6 reduce-scatter.3
  149.3 132.6 reduce-scatter.5
  284.2 132.6 reduce-scatter.7
  442.1 118.9 all-gather.7
  563.1 119.3 all-gather.3
  684.6 119.3 all-gather.5
where the time goes:
time: 838 us
  waiting for transfers between devices  752 us (90%)
  other arithmetic  27 us (3%)
  local copies, waits for them, and re-layouts  26.8 us (3%)
  between operations  16.8 us (2%)
  blocking collectives  14.3 us (2%)
    reduce_scatter x3, waiting for transfers between devices, step(): lax.psum_scatter(t[0], 'dp', scatter_dimension=1, tiled=True)  400 us
    all_gather x3, waiting for transfers between devices, step(): whole = [lax.all_gather(one[0], 'dp', axis=1, tiled=True) for one in new]  350 us
    unnamed x17, local copies, waits for them, and re-layouts  26.8 us
    convert_element_type x3, other arithmetic, adamw(): return ((w - 0.02 * step).astype(jnp.bfloat16), m, v)  18.4 us
  transfers between devices with their start and end apart: 6, of which 6 were waited for; matrix products, arithmetic and copies ran while one was open for 2% of the time, Pallas kernels for 0%

commit v1 on v0

v1 whole, which is shorter than its diff:
```python
import functools

import jax
import jax.numpy as jnp
from jax import lax
from jax.experimental import pallas as pl
from jax.experimental.pallas import tpu as pltpu
from jax.sharding import PartitionSpec as P

MESH = pl.DeviceIdType.MESH
RING = 8
SLOTS = 4
LAG = 2
SHAPES = ((128, 3200, 32, 640), (128, 3200, 32, 640), (400, 1024, 80, 1024))
SUBS = tuple(r // ch for r, _, ch, _ in SHAPES)
FIRST = tuple(4 * sum(SUBS[:k]) for k in range(4))
STEPS = FIRST[3]
OWN = tuple(2 * sum(SUBS[:k]) for k in range(4))
COUNT = 19660800.0
F32, BF16 = jnp.float32, jnp.bfloat16


def pieces(k, body):
    _, cols, ch, pc = SHAPES[k]

    @pl.loop(0, ch // 16)
    def _(r):
        row = pl.multiple_of(r * 16, 16)
        for col in range(0, cols, pc):
            body(row, col)


def kernel(*refs):
    g, w, m, v = (refs[3 * i : 3 * i + 3] for i in range(4))
    out, gown, fac_out = refs[12:15], refs[15:18], refs[18]
    rest = list(refs[19:])

    def take(n):
        got, rest[:n] = tuple(rest[:n]), []
        return got

    inc, pb, wn = take(3), take(3), take(3)
    own_a, own_b, wa, wb, ma, mb, va, vb, acc_a, acc_b, stat = take(11)
    recv1, part, wr, grecv = take(3), take(3), take(3), take(3)
    own_sem, load_sem, psend, fsend, gsend, osend, isend, pwsend, pwrecv, local, stat_send, stat_recv, misc = take(13)

    rep, me = lax.axis_index("rep"), lax.axis_index("dp")
    z, c = me // 2, lax.rem(me, 2)
    dev = lambda zz, cc: (rep, 2 * zz + cc)
    partner = (rep, 2 * z + 1 - c)
    is_end = (z == 0) | (z == 3)
    left_half = z < 2
    zo = jnp.where(left_half, 0, 3)
    zm = jnp.where(left_half, 1, 2)
    zf = 3 - zm

    own = lambda k: own_a if k < 2 else own_b

    def remote(src, dst, send, recv, device):
        return pltpu.make_async_remote_copy(src_ref=src, dst_ref=dst, send_sem=send, recv_sem=recv, device_id=device, device_id_type=MESH)

    def rows(k, b, cc, s):
        r, _, ch, _ = SHAPES[k]
        step = 16
        return pl.ds(pl.multiple_of((2 * b + cc) * r + s * ch, step), SHAPES[k][2])

    def sub(k, s):
        ch = SHAPES[k][2]
        return pl.ds(pl.multiple_of(s * ch, 16), ch)

    barrier = pltpu.get_barrier_semaphore()
    for other in range(1, 8):
        pl.semaphore_signal(barrier, inc=1, device_id=(rep, lax.rem(me + other, 8)), device_id_type=MESH)
    pl.semaphore_wait(barrier, 7)

    def load(j, start):
        for k in range(3):
            @pl.when((j >= OWN[k]) & (j < OWN[k + 1]))
            def _():
                t = j - OWN[k]
                l, s, slot = t // SUBS[k], lax.rem(t, SUBS[k]), lax.rem(j, SLOTS)
                bufs = (wa, ma, va) if k < 2 else (wb, mb, vb)
                srcs = (w[k].at[l, rows(k, z, c, s)], m[k].at[l, sub(k, s)], v[k].at[l, sub(k, s)])
                for i in range(3):
                    copy = pltpu.make_async_copy(srcs[i], bufs[i].at[slot], load_sem.at[i, slot])
                    copy.start() if start else copy.wait()

    place = (z, 3 - z)
    after = (jnp.minimum(z + 1, 3), jnp.maximum(z - 1, 0))

    def where_is(f, k, i):
        t = i - FIRST[k]
        q, s = t // SUBS[k], lax.rem(t, SUBS[k])
        b = q // 2 + 2 if f == 0 else 1 - q // 2
        return b, lax.rem(q, 2), s

    def fetch(f, i):
        for k in range(3):
            @pl.when((i >= FIRST[k]) & (i < FIRST[k + 1]))
            def _():
                b, l, s = where_is(f, k, i)
                slot = lax.rem(i, RING)
                remote(g[k].at[0, l, rows(k, b, 1 - c, s)], pb[k].at[b, l, sub(k, s)], psend.at[k], part[k].at[b, l, s], partner).start()
                pltpu.make_async_copy(g[k].at[0, l, rows(k, b, c, s)], own(k).at[f, slot], own_sem.at[f, slot]).start()

    def advance(f, i):
        for k in range(3):
            @pl.when((i >= FIRST[k]) & (i < FIRST[k + 1]))
            def _():
                b, l, s = where_is(f, k, i)
                slot = lax.rem(i, RING)
                here = (b, l, sub(k, s))
                _, _, _, pc = SHAPES[k]
                acc = acc_a if k < 2 else acc_b
                pltpu.make_async_copy(g[k].at[0, l, rows(k, b, c, s)], own(k).at[f, slot], own_sem.at[f, slot]).wait()
                remote(pb[k].at[here], pb[k].at[here], psend.at[k], part[k].at[b, l, s], partner).wait_recv()
                along = remote(pb[k].at[here], inc[k].at[here], fsend.at[f, k], recv1[k].at[b, l, s], dev(after[f], c))

                def total(row, col, arrived):
                    at = (pl.ds(row, 16), pl.ds(col, pc))
                    to = (b, l, pl.ds(pl.multiple_of(s * SHAPES[k][2] + row, 16), 16), pl.ds(col, pc))
                    sum_ = own(k)[(f, slot, *at)].astype(F32) + pb[k][to].astype(F32)
                    if arrived:
                        sum_ = sum_ + inc[k][to].astype(F32)
                    return to, sum_.astype(BF16)

                @pl.when(place[f] == 0)
                def _():
                    def body(row, col):
                        to, sum_ = total(row, col, False)
                        pb[k][to] = sum_

                    pieces(k, body)

                @pl.when(place[f] > 0)
                def _():
                    along.wait_recv()

                @pl.when((place[f] > 0) & (place[f] < 3))
                def _():
                    def body(row, col):
                        to, sum_ = total(row, col, True)
                        pb[k][to] = sum_

                    pieces(k, body)

                @pl.when(place[f] < 3)
                def _():
                    along.start()

                @pl.when(place[f] == 3)
                def _():
                    def body(row, col):
                        to, sum_ = total(row, col, True)
                        inc[k][to] = sum_
                        rounded = sum_.astype(F32)
                        acc[...] += rounded * rounded

                    pieces(k, body)

    def chunks(k, body):
        @pl.loop(0, 2 * SUBS[k])
        def _(t):
            body(t // SUBS[k], lax.rem(t, SUBS[k]))

    acc_a[...] = jnp.zeros_like(acc_a)
    acc_b[...] = jnp.zeros_like(acc_b)

    @pl.loop(0, RING)
    def _(i):
        for f in range(2):
            fetch(f, i)

    @pl.loop(0, SLOTS)
    def _(j):
        load(j, True)

    @pl.loop(0, STEPS + 3 * LAG)
    def _(step):
        for f in range(2):
            i = step - LAG * place[f]

            @pl.when((i >= 0) & (i < STEPS))
            def _():
                advance(f, i)
                fetch(f, i + RING)

        @pl.when((step == STEPS) & is_end)
        def _():
            for k in range(3):
                def back(l, s):
                    here = inc[k].at[zm, l, sub(k, s)]
                    remote(here, here, gsend.at[k], grecv[k].at[l, s], dev(zm, c)).start()

                chunks(k, back)

    slot_of = lambda zz, cc: jnp.where(zz == 0, 0, 2) + cc

    def each_other(body):
        for other in range(1, 8):
            body(other - 1, (rep, lax.rem(me + other, 8)))

    mine = slot_of(z, c)

    @pl.when(is_end)
    def _():
        stat[mine] = jnp.full((8, 128), jnp.sum(acc_a[...]) + jnp.sum(acc_b[...]), F32)
        each_other(lambda i, d: remote(stat.at[mine], stat.at[mine], stat_send.at[i], stat_recv.at[mine], d).start())

    for source in range(4):
        @pl.when((mine != source) | jnp.logical_not(is_end))
        def _():
            remote(stat.at[source], stat.at[source], stat_send.at[0], stat_recv.at[source], partner).wait_recv()

    squares = stat[0] + stat[1] + stat[2] + stat[3]
    factor = jnp.minimum(1.0, 0.5 * lax.rsqrt(squares / COUNT + 1e-30))
    fac_out[...] = factor
    scale = factor[0:1, 0:1]

    def update(j, send):
        load(j, False)
        for k in range(3):
            @pl.when((j >= OWN[k]) & (j < OWN[k + 1]))
            def _():
                t = j - OWN[k]
                l, s, slot = t // SUBS[k], lax.rem(t, SUBS[k]), lax.rem(j, SLOTS)
                wx, mx, vx = (wa, ma, va) if k < 2 else (wb, mb, vb)
                _, _, ch, pc = SHAPES[k]

                @pl.when(jnp.logical_not(is_end))
                def _():
                    here = inc[k].at[z, l, sub(k, s)]
                    remote(here, here, gsend.at[k], grecv[k].at[l, s], partner).wait_recv()

                def body(row, col):
                    at = (slot, pl.ds(row, 16), pl.ds(col, pc))
                    to = (l, pl.ds(pl.multiple_of(s * ch + row, 16), 16), pl.ds(col, pc))
                    grad = inc[k][(z, *to)].astype(F32) * scale
                    new_m = 0.9 * mx[at] + 0.1 * grad
                    new_v = 0.95 * vx[at] + 0.05 * grad * grad
                    old = wx[at].astype(F32)
                    wn[k][to] = (old - 0.02 * (new_m * lax.rsqrt(new_v + 1e-8) + 0.1 * old)).astype(BF16)

                pieces(k, body)
                src, dst = wn[k].at[l, sub(k, s)], out[k].at[l, rows(k, z, c, s)]
                send(k, l, s, src, dst)
                remote(src, dst, pwsend.at[k], pwrecv.at[k], partner).start()
                pltpu.make_async_copy(src, dst, local.at[k]).start()
        load(j + SLOTS, True)

    def pass_on(k, l, s, b, to_sem, to):
        here = out[k].at[l, rows(k, b, c, s)]
        remote(here, here, gsend.at[k], wr[k].at[b, l, s], partner).wait_recv()
        if to is not None:
            remote(here, here, to_sem.at[k], wr[k].at[b, l, s], to).start()
        remote(here, here, pwsend.at[k], pwrecv.at[k], partner).start()

    def pass_index(j, b, to_sem, to):
        for k in range(3):
            @pl.when((j >= OWN[k]) & (j < OWN[k + 1]))
            def _():
                t = j - OWN[k]
                pass_on(k, t // SUBS[k], lax.rem(t, SUBS[k]), b, to_sem, to)

    @pl.when(is_end)
    def _():
        inward = dev(zm, c)

        @pl.loop(0, OWN[3])
        def _(j):
            update(j, lambda k, l, s, src, dst: remote(src, dst, isend.at[k], wr[k].at[z, l, s], inward).start())

        @pl.loop(0, OWN[3])
        def _(j):
            pass_index(j, zm, None, None)
            pass_index(j, zf, None, None)

        @pl.loop(0, OWN[3])
        def _(j):
            pass_index(j, 3 - zo, None, None)

    @pl.when(jnp.logical_not(is_end))
    def _():
        outward, inward = dev(zo, c), dev(zf, c)

        def both(k, l, s, src, dst):
            remote(src, dst, osend.at[k], wr[k].at[z, l, s], outward).start()
            remote(src, dst, isend.at[k], wr[k].at[z, l, s], inward).start()

        @pl.loop(0, OWN[3] + LAG)
        def _(j):
            @pl.when(j < OWN[3])
            def _():
                update(j, both)

            @pl.when(j >= LAG)
            def _():
                pass_index(j - LAG, zf, osend, outward)

        @pl.loop(0, OWN[3])
        def _(j):
            pass_index(j, zo, isend, inward)
            pass_index(j, 3 - zo, osend, outward)

    for k in range(3):
        pltpu.make_async_copy(inc[k].at[z], gown[k], misc.at[k]).start()

    for k in range(3):
        r = SHAPES[k][0]
        blocks = lambda n: pb[k].at[pl.ds(0, n)]
        sent = lambda n, sem: remote(blocks(n), blocks(n), sem, pwrecv.at[k], partner).wait_send()
        sent(4, psend.at[k])
        for f in range(2):
            @pl.when(place[f] < 3)
            def _():
                sent(2, fsend.at[f, k])

        @pl.when(is_end)
        def _():
            sent(1, gsend.at[k])
            sent(1, isend.at[k])

        @pl.when(jnp.logical_not(is_end))
        def _():
            sent(3, osend.at[k])
            sent(2, isend.at[k])

        sent(4, pwsend.at[k])
        pltpu.make_async_copy(wn[k], gown[k], local.at[k]).wait()
        half = out[k].at[:, pl.ds(0, 4 * r)]
        remote(half, half, gsend.at[k], pwrecv.at[k], partner).wait_recv()
        pltpu.make_async_copy(inc[k].at[z], gown[k], misc.at[k]).wait()

    @pl.when(is_end)
    def _():
        each_other(lambda i, d: remote(stat.at[mine], stat.at[mine], stat_send.at[i], stat_recv.at[mine], d).wait_send())


def exchange(*arrays):
    any_, dma = pl.BlockSpec(memory_space=pl.ANY), pltpu.SemaphoreType.DMA
    whole = [jax.ShapeDtypeStruct((2, 8 * r, n), BF16) for r, n, _, _ in SHAPES]
    block = [jax.ShapeDtypeStruct((2, r, n), BF16) for r, n, _, _ in SHAPES]
    (_, na, ca, pa), (_, nb, cb, pc) = SHAPES[0], SHAPES[2]
    scratch = [pltpu.VMEM((4, 2, r, n), BF16) for r, n, _, _ in SHAPES] * 2
    scratch += [pltpu.VMEM((2, r, n), BF16) for r, n, _, _ in SHAPES]
    scratch += [pltpu.VMEM((2, RING, ca, na), BF16), pltpu.VMEM((2, RING, cb, nb), BF16)]
    for dtype in (BF16, F32, F32):
        scratch += [pltpu.VMEM((SLOTS, ca, na), dtype), pltpu.VMEM((SLOTS, cb, nb), dtype)]
    scratch += [pltpu.VMEM((16, pa), F32), pltpu.VMEM((16, pc), F32), pltpu.VMEM((4, 8, 128), F32)]
    scratch += [dma((4, 2, s)) for s in SUBS] * 3 + [dma((2, s)) for s in SUBS]
    scratch += [dma((2, RING)), dma((3, SLOTS)), dma((3,)), dma((2, 3)), *[dma((3,))] * 6, dma((7,)), dma((4,)), dma((3,))]
    return pl.pallas_call(
        kernel,
        name="exchange",
        out_shape=(*whole, *block, jax.ShapeDtypeStruct((8, 128), F32)),
        in_specs=[any_] * 12,
        out_specs=(*[any_] * 6, pl.BlockSpec(memory_space=pltpu.VMEM)),
        scratch_shapes=scratch,
        compiler_params=pltpu.CompilerParams(collective_id=0, has_side_effects=True, vmem_limit_bytes=67043328),
    )(*arrays)


def solution(mesh):
    def step(*arrays):
        m, v = arrays[6:9], arrays[9:12]
        *rest, factor = exchange(*arrays)
        new, gradients = rest[:3], rest[3:]
        gradients = [g.astype(F32) * factor[0, 0] for g in gradients]
        new_m = [0.9 * one + 0.1 * g for one, g in zip(m, gradients, strict=True)]
        new_v = [0.95 * one + 0.05 * g * g for one, g in zip(v, gradients, strict=True)]
        return (*new, *new_m, *new_v)

    all_of, cut = P(None, None, None), P(None, "dp", None)
    return jax.shard_map(
        step,
        mesh=mesh,
        in_specs=(P(("rep", "dp"), None, None, None),) * 3 + (all_of,) * 3 + (cut,) * 6,
        out_specs=(P("rep", None, None),) * 3 + (P("rep", "dp", None),) * 6,
        check_vma=False,
    )
```

time: 838 us -> 693 us (0.83)
  waiting for transfers between devices: 752 us -> 0 us
  Pallas kernels: 0 us -> 650 us
  between operations: 16.8 us -> 0.78 us
  blocking collectives: 14.3 us -> 0 us
    pallas_call x0 -> x1, Pallas kernels: none -> 650 us  [exchange(): pl.pallas_call(kernel, name='exchange', out_shape=(*whole, *block, jax.Sh...]
    reduce_scatter x3 -> x0, waiting for transfers between devices: 400 us -> none  [step(): lax.psum_scatter(t[0], 'dp', scatter_dimension=1, tiled=True)]
    all_gather x3 -> x0, waiting for transfers between devices: 350 us -> none  [step(): whole = [lax.all_gather(one[0], 'dp', axis=1, tiled=True) for one in new]]
    add x0 -> x2, other arithmetic: none -> 19 us  [step(): 0.95 * one + 0.05 * g * g]
    convert_element_type x3 -> x0, other arithmetic: 18.4 us -> none  [adamw(): return ((w - 0.02 * step).astype(jnp.bfloat16), m, v)]
    psum x1 -> x0, blocking collectives: 14.3 us -> none  [step(): squares = lax.psum(sum((jnp.sum(g * g) for g in gradients)), 'dp')]
    reduce_sum x3 -> x0, other arithmetic: 8.63 us -> none  [step(): squares = lax.psum(sum((jnp.sum(g * g) for g in gradients)), 'dp')]
    unnamed x17 -> x33, local copies, waits for them, and re-layouts: 26.8 us -> 21.8 us
  transfers between devices with their start and end apart: 6 -> 0, of which waited for: 6 -> 0; matrix products, arithmetic and copies ran while one was open for 2% -> 0% of each run, Pallas kernels for 0% -> 0%
where the time goes in v1:
time: 693 us; the launch traced here: 692 us
  Pallas kernels  650 us (94%)
  local copies, waits for them, and re-layouts  23 us (3%)
  other arithmetic  19 us (3%)
    pallas_call x1, Pallas kernels, exchange(): pl.pallas_call(kernel, name='exchange', out_shape=(*whole, *block, jax.Sh...  650 us
    unnamed x33, local copies, waits for them, and re-layouts  21.8 us
    add x2, other arithmetic, step(): 0.95 * one + 0.05 * g * g  19 us

profile of v1, /device:TPU:0, one launch (start us, length us, event | category | flops | bytes accessed | tf_op | source)
XLA Modules:
  0.0 692.3 jit_solution(14229360323523734321)
XLA Ops:
  0.6 649.6 %exchange.1 = (bf16[2,1024,3200]{2,1,0:T(8,128)(2,1)}, bf16[2,1024,3200]{2,1,0:T(8,128)(2,1)}, bf16[2,3200,1024]{2,1,0:T(8,128)(2,1)}, bf16[2,128,3200]{2,1,0:T(...) custom-call(bf16[1,2,1024,3200]{3,2,1,0:T(8,128)(2,1)} %refs_0_.1, ...), custom_call_target="tpu_custom_call" | custom-call | tf_op jit(solution)/shard_map/exchange/pallas_call | solution.py:352
  650.3 1.2 slice.2
  651.5 0.0 copy-start
  651.5 0.0 copy-start.1
  651.5 0.0 copy-start.2
  651.5 0.0 slice-start.8
  651.5 0.0 slice-start.9
  651.5 0.0 slice-start.10
  651.5 12.8 %fusion = (f32[2,128,3200]{2,1,0:T(8,128)}, f32[2,128,3200]{2,1,0:T(8,128)}, f32[2,128,3200]{2,1,0:T(8,128)}, f32[2,128,3200]{2,1,0:T(8,128)}) fusion(f32[2,128,3200]{2,1,0:T(8,128)} %refs_9_.1, bf16[2,128,3200]{2,1,0:T(8,128)(2,1)} %get-tuple-element.19, f32[]{:T(128)} %bitcast, f32[2,128,3200]{2,1,0:T(8,128)} %refs_6_.1, ...), kind=kLoop, calls=%fused_computation.3 | loop fusion | flops 14745600 | bytes 29491204 | tf_op jit(solution)/shard_map/add | solution.py:370
  664.3 0.0 copy-done
  664.3 0.0 copy-done.1
  664.3 0.0 copy-done.2
  664.3 0.0 slice-start.11
  664.3 0.0 slice-start.4
  664.3 0.0 slice-start.5
  664.4 6.2 fusion.2
  670.5 0.0 slice-done.8
  670.5 0.0 slice-done.9
  670.5 0.0 slice-done.10
  670.5 0.0 slice-done.11
  670.5 0.0 slice-start.6
  670.6 0.0 slice-start.7
  670.6 0.0 slice-start
  670.6 0.0 slice-start.1
  670.6 6.6 copy.24
  677.2 0.0 slice-done.4
  677.2 0.0 slice-done.5
  677.2 0.0 slice-done.6
  677.2 1.8 slice-done.7
  679.0 0.0 slice-start.2
  679.0 0.0 slice-start.3
  679.0 6.6 copy.25
  685.7 0.0 slice-done
  685.7 0.0 slice-done.1
  685.7 1.7 slice-done.2
  687.4 0.0 slice-done.3
  687.4 4.9 copy.26
  (3 shorter events, 0.0 us)
Async XLA Ops:
  651.5 12.8 %copy-start = (f32[2,400,1024]{2,1,0:T(8,128)S(1)}, f32[2,400,1024]{2,1,0:T(8,128)}, u32[]{:S(2)}) copy-start(f32[2,400,1024]{2,1,0:T(8,128)} %refs_8_.1) | copy-start | bytes 9830404
  651.5 12.8 %copy-start.1 = (f32[2,400,1024]{2,1,0:T(8,128)S(1)}, f32[2,400,1024]{2,1,0:T(8,128)}, u32[]{:S(2)}) copy-start(f32[2,400,1024]{2,1,0:T(8,128)} %refs_11_.1) | copy-start | bytes 9830404
  651.5 12.9 %copy-start.2 = (bf16[2,400,1024]{2,1,0:T(8,128)(2,1)S(1)}, bf16[2,400,1024]{2,1,0:T(8,128)(2,1)}, u32[]{:S(2)}) copy-start(bf16[2,400,1024]{2,1,0:T(8,128)(2,1)} %get-tuple-element.22) | copy-start | bytes 4915204
  651.5 19.1 %slice-start.8 = ((s8[13107200]{0:T(1024)(128)(4,1)}), s8[4194304]{0:T(1024)(128)(4,1)S(1)}, s32[]{:S(2)}) async-start(s8[13107200]{0:T(1024)(128)(4,1)} %bitcast.5), calls=%async_computation.8 | async-start | bytes 8388608
  651.5 19.1 %slice-start.9 = ((s8[13107200]{0:T(1024)(128)(4,1)}), s8[4194304]{0:T(1024)(128)(4,1)S(1)}, s32[]{:S(2)}) async-start(s8[13107200]{0:T(1024)(128)(4,1)} %bitcast.5), calls=%async_computation.9 | async-start | bytes 8388608
  651.5 19.0 %slice-start.10 = ((s8[13107200]{0:T(1024)(128)(4,1)}), s8[4194304]{0:T(1024)(128)(4,1)S(1)}, s32[]{:S(2)}) async-start(s8[13107200]{0:T(1024)(128)(4,1)} %bitcast.5), calls=%async_computation.10 | async-start | bytes 8388608
  664.3 6.2 slice-start.11
  664.3 12.9 %slice-start.4 = ((s8[13107200]{0:T(1024)(128)(4,1)}), s8[524288]{0:T(1024)(128)(4,1)S(1)}, s32[]{:S(2)}) async-start(s8[13107200]{0:T(1024)(128)(4,1)} %bitcast.3), calls=%async_computation.4 | async-start | bytes 1048576
  664.3 12.9 %slice-start.5 = ((s8[13107200]{0:T(1024)(128)(4,1)}), s8[4194304]{0:T(1024)(128)(4,1)S(1)}, s32[]{:S(2)}) async-start(s8[13107200]{0:T(1024)(128)(4,1)} %bitcast.3), calls=%async_computation.5 | async-start | bytes 8388608
  670.5 6.7 slice-start.6
  670.6 8.5 %slice-start.7 = ((s8[13107200]{0:T(1024)(128)(4,1)}), s8[4194304]{0:T(1024)(128)(4,1)S(1)}, s32[]{:S(2)}) async-start(s8[13107200]{0:T(1024)(128)(4,1)} %bitcast.3), calls=%async_computation.7 | async-start | bytes 8388608
  670.6 15.1 %slice-start = ((s8[13107200]{0:T(1024)(128)(4,1)}), s8[4194304]{0:T(1024)(128)(4,1)S(1)}, s32[]{:S(2)}) async-start(s8[13107200]{0:T(1024)(128)(4,1)} %bitcast.1), calls=%async_computation | async-start | bytes 8388608
  670.6 15.1 %slice-start.1 = ((s8[13107200]{0:T(1024)(128)(4,1)}), s8[4194304]{0:T(1024)(128)(4,1)S(1)}, s32[]{:S(2)}) async-start(s8[13107200]{0:T(1024)(128)(4,1)} %bitcast.1), calls=%async_computation.1 | async-start | bytes 8388608
  679.0 8.4 %slice-start.2 = ((s8[13107200]{0:T(1024)(128)(4,1)}), s8[4194304]{0:T(1024)(128)(4,1)S(1)}, s32[]{:S(2)}) async-start(s8[13107200]{0:T(1024)(128)(4,1)} %bitcast.1), calls=%async_computation.2 | async-start | bytes 8388608
  679.0 8.4 %slice-start.3 = ((s8[13107200]{0:T(1024)(128)(4,1)}), s8[524288]{0:T(1024)(128)(4,1)S(1)}, s32[]{:S(2)}) async-start(s8[13107200]{0:T(1024)(128)(4,1)} %bitcast.1), calls=%async_computation.3 | async-start | bytes 1048576

commit v2 on v1

v2 whole, which is shorter than its diff:
```python
import functools

import jax
import jax.numpy as jnp
from jax import lax
from jax.experimental import pallas as pl
from jax.experimental.pallas import tpu as pltpu
from jax.sharding import PartitionSpec as P

MESH = pl.DeviceIdType.MESH
RING = 8
SLOTS = 4
LAG = 2
PASS_LAG = 3
BEHIND = 16
SHAPES = ((128, 3200, 32, 640), (128, 3200, 32, 640), (400, 1024, 80, 1024))
SUBS = tuple(r // ch for r, _, ch, _ in SHAPES)
FIRST = (0, 4 * SUBS[0], 8 * SUBS[0], 8 * SUBS[0] + 4 * SUBS[2], 8 * SUBS[0] + 6 * SUBS[2])
STEPS = FIRST[4] + LAG
ORDER = (2, 0, 1)
OWN = {2: (0, 2 * SUBS[2]), 0: (2 * SUBS[2], 2 * (SUBS[2] + SUBS[0])), 1: (2 * (SUBS[2] + SUBS[0]), 2 * (SUBS[2] + 2 * SUBS[0]))}
BLOCK = OWN[1][1]
QUARTER = SHAPES[0][0] // 4
COUNT = 19660800.0
F32, BF16 = jnp.float32, jnp.bfloat16


def pieces(k, body):
    _, cols, ch, pc = SHAPES[k]

    @pl.loop(0, ch // 16)
    def _(r):
        row = pl.multiple_of(r * 16, 16)
        for col in range(0, cols, pc):
            body(row, col)


def kernel(*refs):
    g, w, m, v = (refs[3 * i : 3 * i + 3] for i in range(4))
    out, gown, moments, fac_out = refs[12:15], refs[15:18], refs[18:22], refs[22]
    rest = list(refs[23:])

    def take(n):
        got, rest[:n] = tuple(rest[:n]), []
        return got

    inc, pb, wn = take(3), take(3), take(3)
    inc_near, own_a, own_b, wa, wb, ma, mb, va, vb, acc_a, acc_b, stat = take(12)
    recv1, part, wr, grecv = take(3), take(3), take(3), take(2)
    near_recv, own_sem, load_sem, psend, fsend, near_send, gsend, osend, isend, pwsend, pwrecv, local = take(12)
    stat_send, stat_recv, mv_send, mv_recv, mv_fan, mv_all, misc = take(7)

    rep, me = lax.axis_index("rep"), lax.axis_index("dp")
    z, c = me // 2, lax.rem(me, 2)
    dev = lambda zz, cc: (rep, 2 * zz + cc)
    partner = (rep, 2 * z + 1 - c)
    is_end = (z == 0) | (z == 3)
    is_mid = jnp.logical_not(is_end)
    left_half = z < 2
    zo = jnp.where(left_half, 0, 3)
    zm = jnp.where(left_half, 1, 2)
    zf = 3 - zm

    own = lambda k: own_a if k < 2 else own_b

    def remote(src, dst, send, recv, device):
        return pltpu.make_async_remote_copy(src_ref=src, dst_ref=dst, send_sem=send, recv_sem=recv, device_id=device, device_id_type=MESH)

    def rows(k, b, cc, s):
        r, _, ch, _ = SHAPES[k]
        return pl.ds(pl.multiple_of((2 * b + cc) * r + s * ch, 16), ch)

    def sub(k, s):
        ch = SHAPES[k][2]
        return pl.ds(pl.multiple_of(s * ch, 16), ch)

    barrier = pltpu.get_barrier_semaphore()
    for other in range(1, 8):
        pl.semaphore_signal(barrier, inc=1, device_id=(rep, lax.rem(me + other, 8)), device_id_type=MESH)
    for other in range(1, 4):
        pl.semaphore_signal(barrier, inc=1, device_id=(lax.rem(rep + other, 4), me), device_id_type=MESH)
    pl.semaphore_wait(barrier, 10)

    def quarter(ref, which, l):
        return ref.at[l, pl.ds(pl.multiple_of(which * QUARTER, QUARTER), QUARTER)]

    held = (m[0], m[1], v[0], v[1])

    @pl.when(is_mid)
    def _():
        for i in range(4):
            for l in range(2):
                remote(quarter(held[i], rep, l), quarter(moments[i], rep, l), mv_send.at[i], mv_recv.at[i, l], dev(zo, c)).start()

    def spread(j):
        for i in range(4):
            for l in range(2):
                @pl.when(j == 2 * i + l)
                def _():
                    here = quarter(moments[i], rep, l)
                    remote(here, here, mv_send.at[i], mv_recv.at[i, l], partner).wait_recv()
                    for other in range(1, 4):
                        remote(here, here, mv_fan.at[i], mv_all.at[i], (lax.rem(rep + other, 4), me)).start()

    def load(j, b, start):
        for k in ORDER:
            @pl.when((j >= OWN[k][0]) & (j < OWN[k][1]))
            def _():
                t = j - OWN[k][0]
                l, s, slot = t // SUBS[k], lax.rem(t, SUBS[k]), lax.rem(j, SLOTS)
                bufs = (wa, ma, va) if k < 2 else (wb, mb, vb)
                m_, v_ = (m[k], v[k]) if b is z else (moments[k], moments[2 + k]) if k < 2 else (None, None)
                if m_ is None:
                    return
                srcs = (w[k].at[l, rows(k, b, c, s)], m_.at[l, sub(k, s)], v_.at[l, sub(k, s)])
                for i in range(3):
                    copy = pltpu.make_async_copy(srcs[i], bufs[i].at[slot], load_sem.at[i, slot])
                    copy.start() if start else copy.wait()

    place = (z, 3 - z)
    after = (jnp.minimum(z + 1, 3), jnp.maximum(z - 1, 0))
    middle, end, near = (2, 1), (3, 0), (1, 2)

    def where_is(f, q, i):
        k = min(q, 2)
        t = i - FIRST[q]
        u, s = t // SUBS[k], lax.rem(t, SUBS[k])
        if q < 2:
            return k, jnp.where(u < 2, middle[f], end[f]), lax.rem(u, 2), s, True
        if q == 2:
            return k, jnp.where(u < 2, end[f], middle[f]), lax.rem(u, 2), s, (u < 2) | (place[f] < 2)
        return k, near[f], u, s, place[f] < 2

    def each_part(f, i, body):
        for q in range(4):
            k, b, l, s, active = where_is(f, q, i)

            @pl.when((i >= FIRST[q]) & (i < FIRST[q + 1]) & active)
            def _():
                body(q, k, b, l, s, lax.rem(i, RING))

    def fetch(f, i):
        def start(q, k, b, l, s, slot):
            remote(g[k].at[0, l, rows(k, b, 1 - c, s)], pb[k].at[b, l, sub(k, s)], psend.at[k], part[k].at[b, l, s], partner).start()
            pltpu.make_async_copy(g[k].at[0, l, rows(k, b, c, s)], own(k).at[f, slot], own_sem.at[f, slot]).start()

        each_part(f, i, start)

    def advance(f, i):
        def step(q, k, b, l, s, slot):
            here = (b, l, sub(k, s))
            pc = SHAPES[k][3]
            acc = acc_a if k < 2 else acc_b
            pltpu.make_async_copy(g[k].at[0, l, rows(k, b, c, s)], own(k).at[f, slot], own_sem.at[f, slot]).wait()
            remote(pb[k].at[here], pb[k].at[here], psend.at[k], part[k].at[b, l, s], partner).wait_recv()
            along = remote(pb[k].at[here], inc[k].at[here], fsend.at[f, k], recv1[k].at[b, l, s], dev(after[f], c))
            aside = remote(pb[k].at[here], inc_near.at[l, sub(k, s)], near_send, near_recv.at[l, s], dev(after[f], c))

            def total(into, arrived, squares=False):
                def body(row, col):
                    at = (pl.ds(row, 16), pl.ds(col, pc))
                    down = pl.ds(pl.multiple_of(s * SHAPES[k][2] + row, 16), 16)
                    to = (b, l, down, pl.ds(col, pc))
                    sum_ = own(k)[(f, slot, *at)].astype(F32) + pb[k][to].astype(F32)
                    if "line" in arrived:
                        sum_ = sum_ + inc[k][to].astype(F32)
                    if "near" in arrived:
                        sum_ = sum_ + inc_near[(l, down, pl.ds(col, pc))].astype(F32)
                    sum_ = sum_.astype(BF16)
                    into[k][to] = sum_
                    if squares:
                        rounded = sum_.astype(F32)
                        acc[...] += rounded * rounded

                pieces(k, body)

            if q == 3:

                @pl.when(place[f] == 0)
                def _():
                    total(pb, ())
                    aside.start()

                @pl.when(place[f] == 1)
                def _():
                    along.wait_recv()
                    aside.wait_recv()
                    total(inc, ("line", "near"), True)

                return

            @pl.when(place[f] == 0)
            def _():
                total(pb, ())

            @pl.when(place[f] > 0)
            def _():
                along.wait_recv()

            @pl.when((place[f] > 0) & (place[f] < 3))
            def _():
                total(pb, ("line",))

            @pl.when(place[f] < 3)
            def _():
                along.start()

            @pl.when(place[f] == 3)
            def _():
                total(inc, ("line",), True)

        each_part(f, i, step)

    def chunks(k, body):
        @pl.loop(0, 2 * SUBS[k])
        def _(t):
            body(t // SUBS[k], lax.rem(t, SUBS[k]))

    def back(k, l, s):
        here = inc[k].at[zm, l, sub(k, s)]
        remote(here, here, gsend.at[k], grecv[k].at[l, s], dev(zm, c)).start()

    acc_a[...] = jnp.zeros_like(acc_a)
    acc_b[...] = jnp.zeros_like(acc_b)

    @pl.loop(0, RING)
    def _(i):
        for f in range(2):
            fetch(f, i)

    @pl.loop(0, SLOTS)
    def _(j):
        load(j, z, True)

    @pl.loop(0, STEPS)
    def _(step):
        for f in range(2):
            i = step - LAG * place[f] - jnp.where(place[f] == 3, BEHIND, 0)

            @pl.when((i >= 0) & (i < FIRST[4]))
            def _():
                advance(f, i)
                fetch(f, i + RING)

        @pl.when(is_end & (step >= 4) & (lax.rem(step, 2) == 0))
        def _():
            spread(step // 2 - 2)

    def each_other(body):
        for other in range(1, 8):
            body(other - 1, lax.rem(me + other, 8))

    stat[me] = jnp.full((8, 128), jnp.sum(acc_a[...]) + jnp.sum(acc_b[...]), F32)
    each_other(lambda i, d: remote(stat.at[me], stat.at[me], stat_send.at[i], stat_recv.at[me], (rep, d)).start())

    @pl.when(is_end)
    def _():
        for k in range(2):
            chunks(k, functools.partial(back, k))

    each_other(lambda i, d: remote(stat.at[d], stat.at[d], stat_send.at[0], stat_recv.at[d], partner).wait_recv())
    squares = stat[0]
    for source in range(1, 8):
        squares = squares + stat[source]
    factor = jnp.minimum(1.0, 0.5 * lax.rsqrt(squares / COUNT + 1e-30))
    fac_out[...] = factor
    scale = factor[0:1, 0:1]

    def update(j, b, send, arrays=ORDER, last=BLOCK):
        load(j, b, False)
        for k in arrays:
            @pl.when((j >= OWN[k][0]) & (j < OWN[k][1]))
            def _():
                t = j - OWN[k][0]
                l, s, slot = t // SUBS[k], lax.rem(t, SUBS[k]), lax.rem(j, SLOTS)
                wx, mx, vx = (wa, ma, va) if k < 2 else (wb, mb, vb)
                _, _, ch, pc = SHAPES[k]
                which = 0 if b is z else 1

                if k < 2:

                    @pl.when(is_mid)
                    def _():
                        here = inc[k].at[z, l, sub(k, s)]
                        remote(here, here, gsend.at[k], grecv[k].at[l, s], partner).wait_recv()

                def body(row, col):
                    at = (slot, pl.ds(row, 16), pl.ds(col, pc))
                    to = (l, pl.ds(pl.multiple_of(s * ch + row, 16), 16), pl.ds(col, pc))
                    grad = inc[k][(b, *to)].astype(F32) * scale
                    new_m = 0.9 * mx[at] + 0.1 * grad
                    new_v = 0.95 * vx[at] + 0.05 * grad * grad
                    old = wx[at].astype(F32)
                    wn[k][(which, *to)] = (old - 0.02 * (new_m * lax.rsqrt(new_v + 1e-8) + 0.1 * old)).astype(BF16)

                pieces(k, body)
                src, dst = wn[k].at[which, l, sub(k, s)], out[k].at[l, rows(k, b, c, s)]
                send(k, l, s, src, dst)
                remote(src, dst, pwsend.at[k], pwrecv.at[k], partner).start()
                pltpu.make_async_copy(src, dst, local.at[k]).start()

        @pl.when(j + SLOTS < last)
        def _():
            load(j + SLOTS, b, True)

    def pass_index(j, b, to_sem, to, along=(0, 1, 2)):
        for k in ORDER:
            @pl.when((j >= OWN[k][0]) & (j < OWN[k][1]))
            def _():
                t = j - OWN[k][0]
                l, s = t // SUBS[k], lax.rem(t, SUBS[k])
                here = out[k].at[l, rows(k, b, c, s)]
                remote(here, here, gsend.at[k], wr[k].at[b, l, s], partner).wait_recv()
                if to is not None and k in along:
                    remote(here, here, to_sem.at[k], wr[k].at[b, l, s], to).start()
                remote(here, here, pwsend.at[k], pwrecv.at[k], partner).start()

    @pl.when(is_end)
    def _():
        inward = dev(zm, c)

        @pl.loop(0, BLOCK)
        def _(j):
            update(j, z, lambda k, l, s, src, dst: remote(src, dst, isend.at[k], wr[k].at[z, l, s], inward).start())

        for i in range(4):
            three = moments[i].at[:, pl.ds(0, 3 * QUARTER)]
            remote(three, three, mv_fan.at[i], mv_all.at[i], partner).wait_recv()

        @pl.loop(OWN[0][0], OWN[0][0] + SLOTS)
        def _(j):
            load(j, zm, True)

        @pl.loop(OWN[0][0], BLOCK)
        def _(j):
            update(j, zm, lambda *_: None, (0, 1))

        @pl.loop(0, OWN[2][1])
        def _(j):
            pass_index(j, zm, None, None)
            pass_index(j, zf, None, None)

        @pl.loop(OWN[0][0], BLOCK)
        def _(j):
            pass_index(j, zf, None, None)

        @pl.loop(OWN[0][0], BLOCK)
        def _(j):
            pass_index(j, 3 - zo, None, None)

    @pl.when(is_mid)
    def _():
        outward, inward = dev(zo, c), dev(zf, c)

        def both(k, l, s, src, dst):
            if k == 2:
                remote(src, dst, osend.at[k], wr[k].at[z, l, s], outward).start()
            remote(src, dst, isend.at[k], wr[k].at[z, l, s], inward).start()

        @pl.loop(0, BLOCK + PASS_LAG)
        def _(j):
            @pl.when(j < BLOCK)
            def _():
                update(j, z, both)

            @pl.when(j >= PASS_LAG)
            def _():
                pass_index(j - PASS_LAG, zf, osend, outward)

        @pl.loop(0, BLOCK + PASS_LAG)
        def _(j):
            @pl.when(j < BLOCK)
            def _():
                pass_index(j, zo, isend, inward)

            @pl.when(j >= PASS_LAG)
            def _():
                pass_index(j - PASS_LAG, 3 - zo, osend, outward, (0, 1))

    for k in range(3):
        pltpu.make_async_copy(inc[k].at[z], gown[k], misc.at[k]).start()

    for k in range(3):
        r = SHAPES[k][0]
        blocks = lambda n: pb[k].at[pl.ds(0, n)]
        sent = lambda n, sem: remote(blocks(n), blocks(n), sem, pwrecv.at[k], partner).wait_send()
        sent(4, psend.at[k])
        for f in range(2):
            if k < 2:

                @pl.when(place[f] < 3)
                def _():
                    sent(2, fsend.at[f, k])

            else:

                @pl.when(place[f] < 2)
                def _():
                    sent(2, fsend.at[f, k])

                @pl.when(place[f] == 2)
                def _():
                    sent(1, fsend.at[f, k])

        def delivered(blocks_):
            half = out[k].at[:, pl.ds(0, blocks_ * r)]
            remote(half, half, gsend.at[k], pwrecv.at[k], partner).wait_recv()
            sent(blocks_, pwsend.at[k])

        def stored(n):
            pltpu.make_async_copy(pb[k].at[pl.ds(0, n)], pb[k].at[pl.ds(0, n)], local.at[k]).wait()

        @pl.when(is_end)
        def _():
            if k < 2:
                sent(1, gsend.at[k])
            sent(1, isend.at[k])
            delivered(4 if k < 2 else 3)
            stored(2 if k < 2 else 1)

        @pl.when(is_mid)
        def _():
            sent(2, osend.at[k])
            sent(2, isend.at[k])
            delivered(4)
            stored(1)

        pltpu.make_async_copy(inc[k].at[z], gown[k], misc.at[k]).wait()

    each_other(lambda i, d: remote(stat.at[me], stat.at[me], stat_send.at[i], stat_recv.at[me], (rep, d)).wait_send())

    @pl.when(is_end)
    def _():
        remote(inc_near, inc_near, near_send, mv_all.at[0], partner).wait_send()
        for i in range(4):
            three = moments[i].at[:, pl.ds(0, 3 * QUARTER)]
            remote(three, three, mv_fan.at[i], mv_all.at[i], partner).wait_send()

    @pl.when(is_mid)
    def _():
        for i in range(4):
            one = moments[i].at[:, pl.ds(0, QUARTER)]
            remote(one, one, mv_send.at[i], mv_all.at[i], partner).wait_send()


def exchange(*arrays):
    any_, dma = pl.BlockSpec(memory_space=pl.ANY), pltpu.SemaphoreType.DMA
    whole = [jax.ShapeDtypeStruct((2, 8 * r, n), BF16) for r, n, _, _ in SHAPES]
    block = [jax.ShapeDtypeStruct((2, r, n), BF16) for r, n, _, _ in SHAPES]
    moments = [jax.ShapeDtypeStruct((2, *SHAPES[0][:2]), F32)] * 4
    (_, na, ca, pa), (_, nb, cb, pc) = SHAPES[0], SHAPES[2]
    scratch = [pltpu.VMEM((4, 2, r, n), BF16) for r, n, _, _ in SHAPES] * 2
    scratch += [pltpu.VMEM((2 if r == SHAPES[0][0] else 1, 2, r, n), BF16) for r, n, _, _ in SHAPES]
    scratch += [pltpu.VMEM((2, *SHAPES[2][:2]), BF16)]
    scratch += [pltpu.VMEM((2, RING, ca, na), BF16), pltpu.VMEM((2, RING, cb, nb), BF16)]
    for dtype in (BF16, F32, F32):
        scratch += [pltpu.VMEM((SLOTS, ca, na), dtype), pltpu.VMEM((SLOTS, cb, nb), dtype)]
    scratch += [pltpu.VMEM((16, pa), F32), pltpu.VMEM((16, pc), F32), pltpu.VMEM((8, 8, 128), F32)]
    scratch += [dma((4, 2, s)) for s in SUBS] * 3 + [dma((2, s)) for s in SUBS[:2]]
    scratch += [dma((2, SUBS[2])), dma((2, RING)), dma((3, SLOTS)), dma((3,)), dma((2, 3)), dma, *[dma((3,))] * 6]
    scratch += [dma((7,)), dma((8,)), dma((4,)), dma((4, 2)), dma((4,)), dma((4,)), dma((3,))]
    return pl.pallas_call(
        kernel,
        name="exchange",
        out_shape=(*whole, *block, *moments, jax.ShapeDtypeStruct((8, 128), F32)),
        in_specs=[any_] * 12,
        out_specs=(*[any_] * 10, pl.BlockSpec(memory_space=pltpu.VMEM)),
        scratch_shapes=scratch,
        compiler_params=pltpu.CompilerParams(collective_id=0, has_side_effects=True, vmem_limit_bytes=67043328),
    )(*arrays)


DEPTH = 6


def fresh(arrays):
    size = [(x.shape[1] // 4, x.shape[2]) for x in arrays]

    def copy(*refs):
        n = len(arrays)
        src, dst, bufs, get, put = refs[:n], refs[n : 2 * n], refs[2 * n : 2 * n + 2], refs[-2], refs[-1]
        todo = [(k, l, p) for l in range(2) for p in range(4) for k in range(n)]
        slots, used = [], [0, 0]
        for k, _, _ in todo:
            shape = int(size[k] != size[0])
            slots.append((shape, used[shape] % DEPTH))
            used[shape] += 1

        def ends(i):
            (k, l, p), (shape, slot) = todo[i], slots[i]
            at = (l, pl.ds(p * size[k][0], size[k][0]))
            buf = bufs[shape].at[slot]
            return (
                pltpu.make_async_copy(src[k].at[at], buf, get.at[shape, slot]),
                pltpu.make_async_copy(buf, dst[k].at[at], put.at[shape, slot]),
            )

        before = [next((j for j in range(i - 1, -1, -1) if slots[j] == slots[i]), None) for i in range(len(todo))]
        unwaited = set(range(len(todo)))
        ahead = DEPTH - 2
        for i in range(-ahead, len(todo)):
            if i + ahead < len(todo):
                if before[i + ahead] is not None:
                    ends(before[i + ahead])[1].wait()
                    unwaited.discard(before[i + ahead])
                ends(i + ahead)[0].start()
            if i >= 0:
                ends(i)[0].wait()
                ends(i)[1].start()
        for i in sorted(unwaited):
            ends(i)[1].wait()

    any_ = pl.BlockSpec(memory_space=pl.ANY)
    return pl.pallas_call(
        copy,
        name="fresh",
        in_specs=[any_] * len(arrays),
        out_specs=[any_] * len(arrays),
        out_shape=[jax.ShapeDtypeStruct(x.shape, x.dtype) for x in arrays],
        scratch_shapes=[pltpu.VMEM((DEPTH, *size[0]), BF16), pltpu.VMEM((DEPTH, *size[-1]), BF16)]
        + [pltpu.SemaphoreType.DMA((2, DEPTH))] * 2,
        compiler_params=pltpu.CompilerParams(vmem_limit_bytes=2**25),
        cost_estimate=pl.CostEstimate(flops=10**8, bytes_accessed=4 * sum(x.size for x in arrays), transcendentals=0),
    )(*arrays)


def place(whole, blocks, rows, needed):
    size = blocks[0].shape

    def copy(rows_ref, needed_ref, whole_ref, *refs):
        src, dst, buf, get, put = refs[: len(blocks)], refs[len(blocks)], *refs[-3:]

        @pl.when(needed_ref[0] == 1)
        def _():
            ins = [pltpu.make_async_copy(src[i], buf.at[i], get.at[i]) for i in range(len(blocks))]
            outs = [
                pltpu.make_async_copy(buf.at[i], dst.at[:, pl.ds(pl.multiple_of(rows_ref[i], 16), size[1])], put.at[i])
                for i in range(len(blocks))
            ]
            for one in ins:
                one.start()
            for i, one in enumerate(ins):
                one.wait()
                outs[i].start()
            for one in outs:
                one.wait()

    any_, smem = pl.BlockSpec(memory_space=pl.ANY), pl.BlockSpec(memory_space=pltpu.SMEM)
    return pl.pallas_call(
        copy,
        name="place",
        in_specs=[smem, smem] + [any_] * (1 + len(blocks)),
        out_specs=any_,
        out_shape=jax.ShapeDtypeStruct(whole.shape, whole.dtype),
        scratch_shapes=[pltpu.VMEM((len(blocks), *size), whole.dtype)] + [pltpu.SemaphoreType.DMA((len(blocks),))] * 2,
        input_output_aliases={2: 0},
    )(jnp.stack(rows), needed.astype(jnp.int32)[None], whole, *blocks)


def solution(mesh):
    def step(*arrays):
        m, v = arrays[6:9], arrays[9:12]
        *rest, factor = exchange(*arrays)
        new, gradients = rest[:3], rest[3:6]

        me = lax.axis_index("dp")
        z, core = me // 2, lax.rem(me, 2)
        is_end = (z == 0) | (z == 3)
        r, cols = SHAPES[2][:2]
        far = jnp.where(z < 2, 3, 0)
        take = lambda x, cc: lax.dynamic_slice(x, (0, (2 * far + cc) * r, 0), (2, r, cols))
        mine = lax.ppermute(take(new[2], core), "dp", [(2, 0), (3, 1), (4, 6), (5, 7)])

        gradients = [g.astype(F32) * factor[0, 0] for g in gradients]
        new_m = [0.9 * one + 0.1 * g for one, g in zip(m, gradients, strict=True)]
        new_v = [0.95 * one + 0.05 * g * g for one, g in zip(v, gradients, strict=True)]
        whole = fresh(new)
        mine, whole, new_m, new_v = lax.optimization_barrier((mine, whole, new_m, new_v))

        other = lax.ppermute(mine, "dp", [(0, 1), (1, 0), (6, 7), (7, 6)])
        gate, up, down = whole
        down = place(down, (mine, other), [(2 * far + cc) * r for cc in (core, 1 - core)], is_end)
        return (gate, up, down, *new_m, *new_v)

    all_of, cut = P(None, None, None), P(None, "dp", None)
    return jax.shard_map(
        step,
        mesh=mesh,
        in_specs=(P(("rep", "dp"), None, None, None),) * 3 + (all_of,) * 3 + (cut,) * 6,
        out_specs=(P("rep", None, None),) * 3 + (P("rep", "dp", None),) * 6,
        check_vma=False,
    )
```

time: 693 us -> 545 us (0.79)
  Pallas kernels: 650 us -> 513 us
  local copies, waits for them, and re-layouts: 23 us -> 10.5 us
    pallas_call x1 -> x3, Pallas kernels: 650 us -> 513 us  [the longest x1 486 us: exchange(): pl.pallas_call(kernel, name='exchange', out_shape=(*whole, *block, *momen...]
    unnamed x33 -> x22, local copies, waits for them, and re-layouts: 21.8 us -> 7.71 us
  transfers between devices with their start and end apart: 0 -> 2, of which waited for: 0 -> 1; matrix products, arithmetic and copies ran while one was open for 0% -> 3% of each run, Pallas kernels for 0% -> 4%
where the time goes in v2:
time: 545 us; the launch traced here: 544 us
  Pallas kernels  513 us (94%)
  other arithmetic  13.3 us (2%)
  local copies, waits for them, and re-layouts  10.5 us (2%)
    pallas_call x1, Pallas kernels, exchange(): pl.pallas_call(kernel, name='exchange', out_shape=(*whole, *block, *momen...  486 us
    pallas_call x1, Pallas kernels, fresh(): pl.pallas_call(copy, name='fresh', in_specs=[any_] * len(arrays), out_spe...  23.9 us
    add x2, other arithmetic, step(): 0.95 * one + 0.05 * g * g  12.7 us
  transfers between devices with their start and end apart: 2, of which 1 were waited for; matrix products, arithmetic and copies ran while one was open for 3% of the time, Pallas kernels for 4%

profile of v2, /device:TPU:0, one launch (start us, length us, event | category | flops | bytes accessed | tf_op | source)
XLA Modules:
  0.0 544.1 jit_solution(6917959192883501483)
XLA Ops:
  0.7 485.7 %exchange.1 = (bf16[2,1024,3200]{2,1,0:T(8,128)(2,1)}, bf16[2,1024,3200]{2,1,0:T(8,128)(2,1)}, bf16[2,3200,1024]{2,1,0:T(8,128)(2,1)}, bf16[2,128,3200]{2,1,0:T(...) custom-call(bf16[1,2,1024,3200]{3,2,1,0:T(8,128)(2,1)} %refs_0_.1, ...), custom_call_target="tpu_custom_call" | custom-call | tf_op jit(solution)/shard_map/exchange/pallas_call | solution.py:462
  486.4 1.6 constant_dynamic-slice_fusion
  487.9 1.3 collective-permute-start
  489.2 1.2 slice.2
  490.5 0.0 copy-start
  490.5 4.7 copy-done
  495.2 0.0 copy-start.1
  495.2 0.0 copy-start.2
  495.2 0.0 copy-start.7
  495.2 23.9 %fresh.1 = (bf16[2,1024,3200]{2,1,0:T(8,128)(2,1)}, bf16[2,1024,3200]{2,1,0:T(8,128)(2,1)}, bf16[2,3200,1024]{2,1,0:T(8,128)(2,1)}) custom-call(bf16[2,1024,3200]{2,1,0:T(8,128)(2,1)S(1)} %copy-done, bf16[2,1024,3200]{2,1,0:T(8,128)(2,1)} %get-tuple-element.31.refs_1_, bf16[2,3200,1024]{2,1,0:T(8,128)(2,1)} %get-tuple-element.29.refs_2_), custom_call_target="tpu_custom_call" | custom-call | flops 100000000 | bytes 78643200 | tf_op jit(solution)/shard_map/fresh/pallas_call | solution.py:514
  519.1 0.0 copy-done.1
  519.1 0.0 copy-done.2
  519.1 0.0 copy-done.7
  519.1 0.0 copy-start.3
  519.1 0.0 copy-start.4
  519.2 0.0 copy-start.5
  519.2 0.0 copy-start.6
  519.2 0.0 copy-start.9
  519.2 5.8 %fusion.2 = (f32[2,400,1024]{2,1,0:T(8,128)}, f32[2,400,1024]{2,1,0:T(8,128)}) fusion(f32[2,400,1024]{2,1,0:T(8,128)S(1)} %copy-done.2, bf16[2,400,1024]{2,1,0:T(8,128)(2,1)S(1)} %copy-done.7, f32[]{:T(128)} %bitcast, f32[2,400,1024]{2,1,0:T(8,128)S(1)} %copy-done.1), kind=kLoop, calls=%fused_computation.5 | loop fusion | flops 7372800 | bytes 14745604 | tf_op jit(solution)/shard_map/add | solution.py:576
  524.9 0.0 copy-done.3
  525.0 0.0 copy-done.4
  525.0 0.0 copy-done.5
  525.0 1.3 copy-done.6
  526.3 0.4 copy-done.9
  526.7 7.0 %fusion = (f32[2,128,3200]{2,1,0:T(8,128)}, f32[2,128,3200]{2,1,0:T(8,128)}, f32[2,128,3200]{2,1,0:T(8,128)}, f32[2,128,3200]{2,1,0:T(8,128)}) fusion(f32[2,128,3200]{2,1,0:T(8,128)S(1)} %copy-done.5, bf16[2,128,3200]{2,1,0:T(8,128)(2,1)S(1)} %copy-done.9, f32[]{:T(128)} %bitcast, f32[2,128,3200]{2,1,0:T(8,128)S(1)} %copy-done.3, ...), kind=kLoop, calls=%fused_computation.3 | loop fusion | flops 14745600 | bytes 29491204 | tf_op jit(solution)/shard_map/add | solution.py:576
  533.7 0.0 collective-permute-done.refs_0_
  533.7 0.0 copy-start.8
  533.7 1.9 collective-permute-start.1
  535.7 0.6 pad_add_fusion.rows_ref
  536.2 2.9 collective-permute-done.1.refs_1_
  539.1 0.0 copy-start.10
  539.1 0.0 copy-done.8
  539.1 1.2 copy-done.10
  540.3 3.8 place.1
Async XLA Ops:
  487.9 45.8 %collective-permute-start = (bf16[2,400,1024]{2,1,0:T(8,128)(2,1)S(1)}, bf16[2,400,1024]{2,1,0:T(8,128)(2,1)S(1)}, u32[]{:S(2)}, u32[]{:S(2)}) collective-permute-start(bf16[2,400,1024]{2,1,0:T(8,128)(2,1)S(1)} %constant_dynamic-slice_fusion), channel_id=1, source_target_pairs={{2,0},{3,1},{4,6},{5,7},{10,8},{11,9},{12,14},{13,15},{18,16},{19,... | collective-permute-start | bytes 4915208 | tf_op jit(solution)/shard_map/ppermute | solution.py:572
  490.5 4.7 copy-start
  495.2 23.9 %copy-start.1 = (f32[2,400,1024]{2,1,0:T(8,128)S(1)}, f32[2,400,1024]{2,1,0:T(8,128)}, u32[]{:S(2)}) copy-start(f32[2,400,1024]{2,1,0:T(8,128)} %refs_8_.1) | copy-start | bytes 9830404
  495.2 23.9 %copy-start.2 = (f32[2,400,1024]{2,1,0:T(8,128)S(1)}, f32[2,400,1024]{2,1,0:T(8,128)}, u32[]{:S(2)}) copy-start(f32[2,400,1024]{2,1,0:T(8,128)} %refs_11_.1) | copy-start | bytes 9830404
  495.2 23.9 %copy-start.7 = (bf16[2,400,1024]{2,1,0:T(8,128)(2,1)S(1)}, bf16[2,400,1024]{2,1,0:T(8,128)(2,1)}, u32[]{:S(2)}) copy-start(bf16[2,400,1024]{2,1,0:T(8,128)(2,1)} %get-tuple-element.38) | copy-start | bytes 4915204
  519.1 5.8 %copy-start.3 = (f32[2,128,3200]{2,1,0:T(8,128)S(1)}, f32[2,128,3200]{2,1,0:T(8,128)}, u32[]{:S(2)}) copy-start(f32[2,128,3200]{2,1,0:T(8,128)} %refs_6_.1) | copy-start | bytes 9830404
  519.1 5.8 %copy-start.4 = (f32[2,128,3200]{2,1,0:T(8,128)S(1)}, f32[2,128,3200]{2,1,0:T(8,128)}, u32[]{:S(2)}) copy-start(f32[2,128,3200]{2,1,0:T(8,128)} %refs_7_.1) | copy-start | bytes 9830404
  519.2 5.8 %copy-start.5 = (f32[2,128,3200]{2,1,0:T(8,128)S(1)}, f32[2,128,3200]{2,1,0:T(8,128)}, u32[]{:S(2)}) copy-start(f32[2,128,3200]{2,1,0:T(8,128)} %refs_9_.1) | copy-start | bytes 9830404
  519.2 7.1 %copy-start.6 = (f32[2,128,3200]{2,1,0:T(8,128)S(1)}, f32[2,128,3200]{2,1,0:T(8,128)}, u32[]{:S(2)}) copy-start(f32[2,128,3200]{2,1,0:T(8,128)} %refs_10_.1) | copy-start | bytes 9830404
  519.2 7.6 %copy-start.9 = (bf16[2,128,3200]{2,1,0:T(8,128)(2,1)S(1)}, bf16[2,128,3200]{2,1,0:T(8,128)(2,1)}, u32[]{:S(2)}) copy-start(bf16[2,128,3200]{2,1,0:T(8,128)(2,1)} %get-tuple-element.35) | copy-start | bytes 4915204
  533.7 5.4 copy-start.8
  533.7 5.4 collective-permute-start.1
  539.1 1.2 copy-start.10

commit v3 on v2

--- a/solution.py
+++ b/solution.py
@@ -8,6 +8,7 @@
 from jax.sharding import PartitionSpec as P
 
 MESH = pl.DeviceIdType.MESH
+ALL_VMEM = 67043328
 RING = 8
 SLOTS = 4
 LAG = 2
@@ -37,8 +38,8 @@
 
 def kernel(*refs):
     g, w, m, v = (refs[3 * i : 3 * i + 3] for i in range(4))
-    out, gown, moments, fac_out = refs[12:15], refs[15:18], refs[18:22], refs[22]
-    rest = list(refs[23:])
+    out, gown, moments, far, fac_out = refs[12:15], refs[15:18], refs[18:22], refs[22], refs[23]
+    rest = list(refs[24:])
 
     def take(n):
         got, rest[:n] = tuple(rest[:n]), []
@@ -303,21 +304,28 @@
         def _():
             load(j + SLOTS, b, True)
 
-    def pass_index(j, b, to_sem, to, along=(0, 1, 2)):
+    def pass_index(j, b, to_sem, to, hop=None):
         for k in ORDER:
             @pl.when((j >= OWN[k][0]) & (j < OWN[k][1]))
             def _():
                 t = j - OWN[k][0]
                 l, s = t // SUBS[k], lax.rem(t, SUBS[k])
-                here = out[k].at[l, rows(k, b, c, s)]
+                there = out[k].at[l, rows(k, b, c, s)]
+                aside = far.at[l, sub(k, s)] if k == 1 else None
+                here = aside if k == 1 and hop == 3 else there
                 remote(here, here, gsend.at[k], wr[k].at[b, l, s], partner).wait_recv()
-                if to is not None and k in along:
-                    remote(here, here, to_sem.at[k], wr[k].at[b, l, s], to).start()
-                remote(here, here, pwsend.at[k], pwrecv.at[k], partner).start()
+                if to is not None and not (k == 1 and hop == 3):
+                    remote(here, aside if k == 1 and hop == 2 else there, to_sem.at[k], wr[k].at[b, l, s], to).start()
+                remote(here, there, pwsend.at[k], pwrecv.at[k], partner).start()
+
+    def keep():
+        for k in range(3):
+            pltpu.make_async_copy(inc[k].at[z], gown[k], misc.at[k]).start()
 
     @pl.when(is_end)
     def _():
         inward = dev(zm, c)
+        keep()
 
         @pl.loop(0, BLOCK)
         def _(j):
@@ -344,7 +352,7 @@
         def _(j):
             pass_index(j, zf, None, None)
 
-        @pl.loop(OWN[0][0], BLOCK)
+        @pl.loop(0, OWN[0][1])
         def _(j):
             pass_index(j, 3 - zo, None, None)
 
@@ -367,18 +375,17 @@
             def _():
                 pass_index(j - PASS_LAG, zf, osend, outward)
 
+        keep()
+
         @pl.loop(0, BLOCK + PASS_LAG)
         def _(j):
             @pl.when(j < BLOCK)
             def _():
-                pass_index(j, zo, isend, inward)
+                pass_index(j, zo, isend, inward, 2)
 
             @pl.when(j >= PASS_LAG)
             def _():
-                pass_index(j - PASS_LAG, 3 - zo, osend, outward, (0, 1))
-
-    for k in range(3):
-        pltpu.make_async_copy(inc[k].at[z], gown[k], misc.at[k]).start()
+                pass_index(j - PASS_LAG, 3 - zo, osend, outward, 3)
 
     for k in range(3):
         r = SHAPES[k][0]
@@ -415,12 +422,12 @@
             if k < 2:
                 sent(1, gsend.at[k])
             sent(1, isend.at[k])
-            delivered(4 if k < 2 else 3)
+            delivered(3 if k == 1 else 4)
             stored(2 if k < 2 else 1)
 
         @pl.when(is_mid)
         def _():
-            sent(2, osend.at[k])
+            sent(1 if k == 1 else 3 if k == 2 else 2, osend.at[k])
             sent(2, isend.at[k])
             delivered(4)
             stored(1)
@@ -462,125 +469,183 @@
     return pl.pallas_call(
         kernel,
         name="exchange",
-        out_shape=(*whole, *block, *moments, jax.ShapeDtypeStruct((8, 128), F32)),
+        out_shape=(*whole, *block, *moments, block[1], jax.ShapeDtypeStruct((8, 128), F32)),
         in_specs=[any_] * 12,
-        out_specs=(*[any_] * 10, pl.BlockSpec(memory_space=pltpu.VMEM)),
+        out_specs=(*[any_] * 11, pl.BlockSpec(memory_space=pltpu.VMEM)),
         scratch_shapes=scratch,
-        compiler_params=pltpu.CompilerParams(collective_id=0, has_side_effects=True, vmem_limit_bytes=67043328),
+        compiler_params=pltpu.CompilerParams(collective_id=0, has_side_effects=True, vmem_limit_bytes=ALL_VMEM),
     )(*arrays)
 
 
 DEPTH = 6
-
-
-def fresh(arrays):
-    size = [(x.shape[1] // 4, x.shape[2]) for x in arrays]
-
-    def copy(*refs):
-        n = len(arrays)
-        src, dst, bufs, get, put = refs[:n], refs[n : 2 * n], refs[2 * n : 2 * n + 2], refs[-2], refs[-1]
-        todo = [(k, l, p) for l in range(2) for p in range(4) for k in range(n)]
-        slots, used = [], [0, 0]
-        for k, _, _ in todo:
-            shape = int(size[k] != size[0])
-            slots.append((shape, used[shape] % DEPTH))
-            used[shape] += 1
-
-        def ends(i):
-            (k, l, p), (shape, slot) = todo[i], slots[i]
-            at = (l, pl.ds(p * size[k][0], size[k][0]))
-            buf = bufs[shape].at[slot]
-            return (
-                pltpu.make_async_copy(src[k].at[at], buf, get.at[shape, slot]),
-                pltpu.make_async_copy(buf, dst[k].at[at], put.at[shape, slot]),
-            )
+MOMENT_DEPTH = 8
+
+
+def finish(copies, sets, factor):
+    nc, ns = len(copies), len(sets)
+    size = [(x.shape[1] // 4, x.shape[2]) for x in copies]
+    tall = [m.shape[1] // (4 if m.shape[1] % 64 == 0 else 5) for m, _, _ in sets]
+    shapes = sorted(set(size), reverse=True)
+    kinds = sorted({(t, m.shape[2]) for t, (m, _, _) in zip(tall, sets, strict=True)})
+    todo = [("copy", k, l, p) for l in range(2) for p in range(4) for k in range(nc)]
+    more = [("moment", k, l, p) for l in range(2) for k in range(ns) for p in range(sets[k][0].shape[1] // tall[k])]
+    todo = [x for _, x in sorted([((i + 0.5) / len(todo), x) for i, x in enumerate(todo)] + [((i + 0.5) / len(more), x) for i, x in enumerate(more)])]
+
+    def run(*refs):
+        fac, refs = refs[0], list(refs[1:])
+
+        def take(n):
+            got, refs[:n] = tuple(refs[:n]), []
+            return got
+
+        src, ms, vs, gs, dst, new_m, new_v = (take(n) for n in (nc, ns, ns, ns, nc, ns, ns))
+        bufs = take(len(shapes))
+        mb, vb, gb = (take(len(kinds)) for _ in range(3))
+        get, put = take(2) if nc else (None, None)
+        mget, mput = take(2)
+        scale = fac[0:1, 0:1]
+        used, slots = {}, []
+        for kind, k, _, _ in todo:
+            shape = (kind, shapes.index(size[k]) if kind == "copy" else kinds.index((tall[k], sets[k][0].shape[2])))
+            n = used.get(shape, 0)
+            used[shape] = n + 1
+            slots.append((*shape, n % (DEPTH if kind == "copy" else MOMENT_DEPTH)))
+
+        def moves(i, way):
+            (kind, k, l, p), (_, shape, slot) = todo[i], slots[i]
+            if kind == "copy":
+                at = (l, pl.ds(p * size[k][0], size[k][0]))
+                buf = bufs[shape].at[slot]
+                pairs = [(src[k].at[at], buf, get.at[shape, slot])] if way == 0 else [(buf, dst[k].at[at], put.at[shape, slot])]
+            else:
+                at = (l, pl.ds(p * tall[k], tall[k]))
+                held = [x[shape].at[slot] for x in (mb, vb, gb)]
+                if way == 0:
+                    pairs = [(x[k].at[at], held[n], mget.at[shape, n, slot]) for n, x in enumerate((ms, vs, gs))]
+                else:
+                    pairs = [(held[n], x[k].at[at], mput.at[shape, n, slot]) for n, x in enumerate((new_m, new_v))]
+            return [pltpu.make_async_copy(*pair) for pair in pairs]
+
+        def start(i, way):
+            for one in moves(i, way):
+                one.start()
+
+        def wait(i, way):
+            for one in moves(i, way):
+                one.wait()
+
+        def compute(i):
+            (kind, k, _, _), (_, shape, slot) = todo[i], slots[i]
+            if kind == "copy":
+                return
+            wide = 640 if sets[k][0].shape[2] % 640 == 0 else 1024
+
+            @pl.loop(0, tall[k] // 16)
+            def _(r):
+                for col in range(0, sets[k][0].shape[2], wide):
+                    at = (slot, pl.ds(pl.multiple_of(r * 16, 16), 16), pl.ds(col, wide))
+                    grad = gb[shape][at].astype(F32) * scale
+                    mb[shape][at] = 0.9 * mb[shape][at] + 0.1 * grad
+                    vb[shape][at] = 0.95 * vb[shape][at] + 0.05 * grad * grad
 
         before = [next((j for j in range(i - 1, -1, -1) if slots[j] == slots[i]), None) for i in range(len(todo))]
-        unwaited = set(range(len(todo)))
-        ahead = DEPTH - 2
+        ahead = min([i - j for i, j in enumerate(before) if j is not None], default=len(todo) + 2) - 2
+        open_ = set(range(len(todo)))
         for i in range(-ahead, len(todo)):
-            if i + ahead < len(todo):
-                if before[i + ahead] is not None:
-                    ends(before[i + ahead])[1].wait()
-                    unwaited.discard(before[i + ahead])
-                ends(i + ahead)[0].start()
+            n = i + ahead
+            if n < len(todo):
+                if before[n] is not None:
+                    wait(before[n], 1)
+                    open_.discard(before[n])
+                start(n, 0)
             if i >= 0:
-                ends(i)[0].wait()
-                ends(i)[1].start()
-        for i in sorted(unwaited):
-            ends(i)[1].wait()
+                wait(i, 0)
+                compute(i)
+                start(i, 1)
+        for i in sorted(open_):
+            wait(i, 1)
+
+    any_, dma = pl.BlockSpec(memory_space=pl.ANY), pltpu.SemaphoreType.DMA
+    ms, vs, gs = ([x[n] for x in sets] for n in range(3))
+    outs = [jax.ShapeDtypeStruct(x.shape, x.dtype) for x in (*copies, *ms, *vs)]
+    scratch = [pltpu.VMEM((DEPTH, *x), BF16) for x in shapes]
+    for dtype in (F32, F32, BF16):
+        scratch += [pltpu.VMEM((MOMENT_DEPTH, *x), dtype) for x in kinds]
+    if nc:
+        scratch += [dma((len(shapes), DEPTH))] * 2
+    scratch += [dma((len(kinds), 3, MOMENT_DEPTH)), dma((len(kinds), 2, MOMENT_DEPTH))]
+    moved = sum(4 * x.size for x in copies) + sum(18 * x.size for x in ms)
+    got = pl.pallas_call(
+        run,
+        name="finish",
+        in_specs=[pl.BlockSpec(memory_space=pltpu.VMEM)] + [any_] * (nc + 3 * ns),
+        out_specs=[any_] * len(outs),
+        out_shape=outs,
+        scratch_shapes=scratch,
+        compiler_params=pltpu.CompilerParams(vmem_limit_bytes=ALL_VMEM),
+        cost_estimate=pl.CostEstimate(flops=2 * moved, bytes_accessed=moved, transcendentals=0),
+    )(factor, *copies, *ms, *vs, *gs)
+    return got[:nc], got[nc : nc + ns], got[nc + ns :]
+
+
+def fill(whole, far, mine, other):
+    size = far.shape
+
+    def copy(whole_ref, far_ref, mine_ref, other_ref, out_ref, buf, get, put):
+        me = lax.axis_index("dp")
+        z, core = me // 2, lax.rem(me, 2)
+        is_end = (z == 0) | (z == 3)
+        block = jnp.where(z < 2, 3, 0)
+
+        def move(sources):
+            first = [(2 * block + cc) * size[1] for cc in (core, 1 - core)]
+            ins = [pltpu.make_async_copy(src, buf.at[i], get.at[i]) for i, src in enumerate(sources)]
+            for one in ins:
+                one.start()
+            outs = []
+            for i, one in enumerate(ins):
+                one.wait()
+                outs.append(pltpu.make_async_copy(buf.at[i], out_ref.at[:, pl.ds(pl.multiple_of(first[i], 16), size[1])], put.at[i]))
+                outs[i].start()
+            for one in outs:
+                one.wait()
+
+        @pl.when(is_end)
+        def _():
+            move((mine_ref, other_ref))
+
+        @pl.when(jnp.logical_not(is_end))
+        def _():
+            move((far_ref,))
 
     any_ = pl.BlockSpec(memory_space=pl.ANY)
     return pl.pallas_call(
         copy,
-        name="fresh",
-        in_specs=[any_] * len(arrays),
-        out_specs=[any_] * len(arrays),
-        out_shape=[jax.ShapeDtypeStruct(x.shape, x.dtype) for x in arrays],
-        scratch_shapes=[pltpu.VMEM((DEPTH, *size[0]), BF16), pltpu.VMEM((DEPTH, *size[-1]), BF16)]
-        + [pltpu.SemaphoreType.DMA((2, DEPTH))] * 2,
-        compiler_params=pltpu.CompilerParams(vmem_limit_bytes=2**25),
-        cost_estimate=pl.CostEstimate(flops=10**8, bytes_accessed=4 * sum(x.size for x in arrays), transcendentals=0),
-    )(*arrays)
-
-
-def place(whole, blocks, rows, needed):
-    size = blocks[0].shape
-
-    def copy(rows_ref, needed_ref, whole_ref, *refs):
-        src, dst, buf, get, put = refs[: len(blocks)], refs[len(blocks)], *refs[-3:]
-
-        @pl.when(needed_ref[0] == 1)
-        def _():
-            ins = [pltpu.make_async_copy(src[i], buf.at[i], get.at[i]) for i in range(len(blocks))]
-            outs = [
-                pltpu.make_async_copy(buf.at[i], dst.at[:, pl.ds(pl.multiple_of(rows_ref[i], 16), size[1])], put.at[i])
-                for i in range(len(blocks))
-            ]
-            for one in ins:
-                one.start()
-            for i, one in enumerate(ins):
-                one.wait()
-                outs[i].start()
-            for one in outs:
-                one.wait()
-
-    any_, smem = pl.BlockSpec(memory_space=pl.ANY), pl.BlockSpec(memory_space=pltpu.SMEM)
-    return pl.pallas_call(
-        copy,
-        name="place",
-        in_specs=[smem, smem] + [any_] * (1 + len(blocks)),
+        name="fill",
+        in_specs=[any_] * 4,
         out_specs=any_,
         out_shape=jax.ShapeDtypeStruct(whole.shape, whole.dtype),
-        scratch_shapes=[pltpu.VMEM((len(blocks), *size), whole.dtype)] + [pltpu.SemaphoreType.DMA((len(blocks),))] * 2,
-        input_output_aliases={2: 0},
-    )(jnp.stack(rows), needed.astype(jnp.int32)[None], whole, *blocks)
+        scratch_shapes=[pltpu.VMEM((2, *size), whole.dtype)] + [pltpu.SemaphoreType.DMA((2,))] * 2,
+        input_output_aliases={0: 0},
+        compiler_params=pltpu.CompilerParams(vmem_limit_bytes=ALL_VMEM),
+    )(whole, far, mine, other)
 
 
 def solution(mesh):
     def step(*arrays):
         m, v = arrays[6:9], arrays[9:12]
         *rest, factor = exchange(*arrays)
-        new, gradients = rest[:3], rest[3:6]
-
-        me = lax.axis_index("dp")
-        z, core = me // 2, lax.rem(me, 2)
-        is_end = (z == 0) | (z == 3)
-        r, cols = SHAPES[2][:2]
-        far = jnp.where(z < 2, 3, 0)
-        take = lambda x, cc: lax.dynamic_slice(x, (0, (2 * far + cc) * r, 0), (2, r, cols))
-        mine = lax.ppermute(take(new[2], core), "dp", [(2, 0), (3, 1), (4, 6), (5, 7)])
-
-        gradients = [g.astype(F32) * factor[0, 0] for g in gradients]
-        new_m = [0.9 * one + 0.1 * g for one, g in zip(m, gradients, strict=True)]
-        new_v = [0.95 * one + 0.05 * g * g for one, g in zip(v, gradients, strict=True)]
-        whole = fresh(new)
+        new, gradients, far = rest[:3], rest[3:6], rest[10]
+
+        mine = lax.ppermute(far, "dp", [(2, 0), (3, 1), (4, 6), (5, 7)])
+        sets = list(zip(m, v, gradients, strict=True))
+        whole, new_m, new_v = finish(new, sets[:2], factor)
         mine, whole, new_m, new_v = lax.optimization_barrier((mine, whole, new_m, new_v))
-
         other = lax.ppermute(mine, "dp", [(0, 1), (1, 0), (6, 7), (7, 6)])
+        _, last_m, last_v = finish([], sets[2:], factor)
         gate, up, down = whole
-        down = place(down, (mine, other), [(2 * far + cc) * r for cc in (core, 1 - core)], is_end)
-        return (gate, up, down, *new_m, *new_v)
+        up, other, last_m, last_v = lax.optimization_barrier((up, other, last_m, last_v))
+        return (gate, fill(up, far, mine, other), down, *new_m, *last_m, *new_v, *last_v)
 
     all_of, cut = P(None, None, None), P(None, "dp", None)
     return jax.shard_map(

time: 545 us -> 531 us (0.974)
  other arithmetic: 13.3 us -> 0 us
  Pallas kernels: 513 us -> 525 us
  local copies, waits for them, and re-layouts: 10.5 us -> 0 us
    pallas_call x2 -> x3, Pallas kernels: 27.7 us -> 48.1 us  [the longest x2 44.9 us: finish(): pl.pallas_call(run, name='finish', in_specs=[pl.BlockSpec(memory_space=pl...]
    add x2 -> x0, other arithmetic: 12.7 us -> none  [step(): 0.95 * one + 0.05 * g * g]
    pallas_call x1, Pallas kernels: 486 us -> 477 us  [exchange(): pl.pallas_call(kernel, name='exchange', out_shape=(*whole, *block, *momen...]
    unnamed x22 -> x0, local copies, waits for them, and re-layouts: 7.71 us -> none
  transfers between devices with their start and end apart: 2 -> 2, of which waited for: 1 -> 1; matrix products, arithmetic and copies ran while one was open for 3% -> 0% of each run, Pallas kernels for 4% -> 8%
where the time goes in v3:
time: 531 us; the launch traced here: 530 us
  Pallas kernels  525 us (99%)
    pallas_call x1, Pallas kernels, exchange(): pl.pallas_call(kernel, name='exchange', out_shape=(*whole, *block, *momen...  477 us
    pallas_call x2, Pallas kernels, finish(): pl.pallas_call(run, name='finish', in_specs=[pl.BlockSpec(memory_space=pl...  44.9 us
  transfers between devices with their start and end apart: 2, of which 1 were waited for; matrix products, arithmetic and copies ran while one was open for 0% of the time, Pallas kernels for 8%

profile of v3, /device:TPU:0, one launch (start us, length us, event | category | flops | bytes accessed | tf_op | source)
XLA Modules:
  0.0 530.4 jit_solution(8848566046591869033)
XLA Ops:
  0.6 477.3 %exchange.1 = (bf16[2,1024,3200]{2,1,0:T(8,128)(2,1)}, bf16[2,1024,3200]{2,1,0:T(8,128)(2,1)}, bf16[2,3200,1024]{2,1,0:T(8,128)(2,1)}, bf16[2,128,3200]{2,1,0:T(...) custom-call(bf16[1,2,1024,3200]{3,2,1,0:T(8,128)(2,1)} %refs_0_.1, ...), custom_call_target="tpu_custom_call" | custom-call | tf_op jit(solution)/shard_map/exchange/pallas_call | solution.py:469
  477.9 1.3 collective-permute-start
  479.2 37.7 %finish.2 = (bf16[2,1024,3200]{2,1,0:T(8,128)(2,1)}, bf16[2,1024,3200]{2,1,0:T(8,128)(2,1)}, bf16[2,3200,1024]{2,1,0:T(8,128)(2,1)}, f32[2,128,3200]{2,1,0:T(8,1...) custom-call(f32[8,128]{1,0:T(8,128)} %get-tuple-element.39.refs_0_, ...), custom_call_target="tpu_custom_call" | custom-call | flops 216268800 | bytes 108134400 | tf_op jit(solution)/shard_map/finish/pallas_call | solution.py:578
  516.9 1.2 collective-permute-done.mine_ref
  518.1 1.9 collective-permute-start.1
  520.0 7.2 %finish.3 = (f32[2,400,1024]{2,1,0:T(8,128)}, f32[2,400,1024]{2,1,0:T(8,128)}) custom-call(f32[8,128]{1,0:T(8,128)} %get-tuple-element.39.refs_0_, f32[2,400,1024]{2,1,0:T(8,128)} %refs_1_.3, f32[2,400,1024]{2,1,0:T(8,128)} %refs_2_.3, bf16[2,400,1024]{2,1,0:T(8,128)(2,1)} %get-tuple-element.55.refs_3_), custom_call_target="tpu_custom_call" | custom-call | flops 29491200 | bytes 14745600 | tf_op jit(solution)/shard_map/finish/pallas_call | solution.py:578
  527.2 0.0 collective-permute-done.1.other_ref
  527.2 3.2 fill.1
Async XLA Ops:
  477.9 40.1 %collective-permute-start = (bf16[2,128,3200]{2,1,0:T(8,128)(2,1)}, bf16[2,128,3200]{2,1,0:T(8,128)(2,1)}, u32[]{:S(2)}, u32[]{:S(2)}) collective-permute-start(bf16[2,128,3200]{2,1,0:T(8,128)(2,1)} %get-tuple-element.38.far_ref), channel_id=1, source_target_pairs={{2,0},{3,1},{4,6},{5,7},{10,8},{11,9},{12,14},{13,15},{18,16},{19,... | collective-permute-start | bytes 4915208 | tf_op jit(solution)/shard_map/ppermute | solution.py:640
  518.1 9.2 %collective-permute-start.1 = (bf16[2,128,3200]{2,1,0:T(8,128)(2,1)}, bf16[2,128,3200]{2,1,0:T(8,128)(2,1)}, u32[]{:S(2)}, u32[]{:S(2)}) collective-permute-start(bf16[2,128,3200]{2,1,0:T(8,128)(2,1)} %collective-permute-done.mine_ref), channel_id=1, source_target_pairs={{0,1},{1,0},{6,7},{7,6},{8,9},{9,8},{14,15},{15,14},{16,17},{17,16... | collective-permute-start | bytes 4915208 | tf_op jit(solution)/shard_map/ppermute | solution.py:644

commit v4 on v3

--- a/solution.py
+++ b/solution.py
@@ -9,6 +9,7 @@
 
 MESH = pl.DeviceIdType.MESH
 ALL_VMEM = 67043328
+TILE = 16
 RING = 8
 SLOTS = 4
 LAG = 2
@@ -26,12 +27,16 @@
 F32, BF16 = jnp.float32, jnp.bfloat16
 
 
+def tiled(row):
+    return pl.multiple_of(row, TILE)
+
+
 def pieces(k, body):
     _, cols, ch, pc = SHAPES[k]
 
-    @pl.loop(0, ch // 16)
+    @pl.loop(0, ch // TILE)
     def _(r):
-        row = pl.multiple_of(r * 16, 16)
+        row = tiled(r * TILE)
         for col in range(0, cols, pc):
             body(row, col)
 
@@ -69,11 +74,11 @@
 
     def rows(k, b, cc, s):
         r, _, ch, _ = SHAPES[k]
-        return pl.ds(pl.multiple_of((2 * b + cc) * r + s * ch, 16), ch)
+        return pl.ds(tiled((2 * b + cc) * r + s * ch), ch)
 
     def sub(k, s):
         ch = SHAPES[k][2]
-        return pl.ds(pl.multiple_of(s * ch, 16), ch)
+        return pl.ds(tiled(s * ch), ch)
 
     barrier = pltpu.get_barrier_semaphore()
     for other in range(1, 8):
@@ -159,8 +164,8 @@
 
             def total(into, arrived, squares=False):
                 def body(row, col):
-                    at = (pl.ds(row, 16), pl.ds(col, pc))
-                    down = pl.ds(pl.multiple_of(s * SHAPES[k][2] + row, 16), 16)
+                    at = (pl.ds(row, TILE), pl.ds(col, pc))
+                    down = pl.ds(tiled(s * SHAPES[k][2] + row), TILE)
                     to = (b, l, down, pl.ds(col, pc))
                     sum_ = own(k)[(f, slot, *at)].astype(F32) + pb[k][to].astype(F32)
                     if "line" in arrived:
@@ -286,8 +291,8 @@
                         remote(here, here, gsend.at[k], grecv[k].at[l, s], partner).wait_recv()
 
                 def body(row, col):
-                    at = (slot, pl.ds(row, 16), pl.ds(col, pc))
-                    to = (l, pl.ds(pl.multiple_of(s * ch + row, 16), 16), pl.ds(col, pc))
+                    at = (slot, pl.ds(row, TILE), pl.ds(col, pc))
+                    to = (l, pl.ds(tiled(s * ch + row), TILE), pl.ds(col, pc))
                     grad = inc[k][(b, *to)].astype(F32) * scale
                     new_m = 0.9 * mx[at] + 0.1 * grad
                     new_v = 0.95 * vx[at] + 0.05 * grad * grad
@@ -478,7 +483,7 @@
 
 
 DEPTH = 6
-MOMENT_DEPTH = 8
+MOMENT_DEPTH = 10
 
 
 def finish(copies, sets, factor):
@@ -540,10 +545,10 @@
                 return
             wide = 640 if sets[k][0].shape[2] % 640 == 0 else 1024
 
-            @pl.loop(0, tall[k] // 16)
+            @pl.loop(0, tall[k] // TILE)
             def _(r):
                 for col in range(0, sets[k][0].shape[2], wide):
-                    at = (slot, pl.ds(pl.multiple_of(r * 16, 16), 16), pl.ds(col, wide))
+                    at = (slot, pl.ds(tiled(r * TILE), TILE), pl.ds(col, wide))
                     grad = gb[shape][at].astype(F32) * scale
                     mb[shape][at] = 0.9 * mb[shape][at] + 0.1 * grad
                     vb[shape][at] = 0.95 * vb[shape][at] + 0.05 * grad * grad
@@ -605,7 +610,7 @@
             outs = []
             for i, one in enumerate(ins):
                 one.wait()
-                outs.append(pltpu.make_async_copy(buf.at[i], out_ref.at[:, pl.ds(pl.multiple_of(first[i], 16), size[1])], put.at[i]))
+                outs.append(pltpu.make_async_copy(buf.at[i], out_ref.at[:, pl.ds(tiled(first[i]), size[1])], put.at[i]))
                 outs[i].start()
             for one in outs:
                 one.wait()
@@ -647,11 +652,11 @@
         up, other, last_m, last_v = lax.optimization_barrier((up, other, last_m, last_v))
         return (gate, fill(up, far, mine, other), down, *new_m, *last_m, *new_v, *last_v)
 
-    all_of, cut = P(None, None, None), P(None, "dp", None)
+    all_of, cut = P(), P(None, "dp")
     return jax.shard_map(
         step,
         mesh=mesh,
-        in_specs=(P(("rep", "dp"), None, None, None),) * 3 + (all_of,) * 3 + (cut,) * 6,
-        out_specs=(P("rep", None, None),) * 3 + (P("rep", "dp", None),) * 6,
+        in_specs=(P(("rep", "dp")),) * 3 + (all_of,) * 3 + (cut,) * 6,
+        out_specs=(P("rep"),) * 3 + (P("rep", "dp"),) * 6,
         check_vma=False,
     )

time: 531 us -> 531 us (level)
  no operation moved by 1% of the time
where the time goes in v4:
time: 531 us; the launch traced here: 530 us
  Pallas kernels  525 us (99%)
    pallas_call x1, Pallas kernels, exchange(): pl.pallas_call(kernel, name='exchange', out_shape=(*whole, *block, *momen...  477 us
    pallas_call x2, Pallas kernels, finish(): pl.pallas_call(run, name='finish', in_specs=[pl.BlockSpec(memory_space=pl...  44.8 us
  transfers between devices with their start and end apart: 2, of which 1 were waited for; matrix products, arithmetic and copies ran while one was open for 0% of the time, Pallas kernels for 8%

profile of v4, /device:TPU:0, one launch (start us, length us, event | category | flops | bytes accessed | tf_op | source)
XLA Modules:
  0.0 530.2 jit_solution(7307143825746910825)
XLA Ops:
  0.6 477.3 %exchange.1 = (bf16[2,1024,3200]{2,1,0:T(8,128)(2,1)}, bf16[2,1024,3200]{2,1,0:T(8,128)(2,1)}, bf16[2,3200,1024]{2,1,0:T(8,128)(2,1)}, bf16[2,128,3200]{2,1,0:T(...) custom-call(bf16[1,2,1024,3200]{3,2,1,0:T(8,128)(2,1)} %refs_0_.1, ...), custom_call_target="tpu_custom_call" | custom-call | tf_op jit(solution)/shard_map/exchange/pallas_call | solution.py:474
  477.9 1.3 collective-permute-start
  479.2 37.8 %finish.2 = (bf16[2,1024,3200]{2,1,0:T(8,128)(2,1)}, bf16[2,1024,3200]{2,1,0:T(8,128)(2,1)}, bf16[2,3200,1024]{2,1,0:T(8,128)(2,1)}, f32[2,128,3200]{2,1,0:T(8,1...) custom-call(f32[8,128]{1,0:T(8,128)} %get-tuple-element.39.refs_0_, ...), custom_call_target="tpu_custom_call" | custom-call | flops 216268800 | bytes 108134400 | tf_op jit(solution)/shard_map/finish/pallas_call | solution.py:583
  517.0 1.1 collective-permute-done.mine_ref
  518.1 1.9 collective-permute-start.1
  520.0 7.0 %finish.3 = (f32[2,400,1024]{2,1,0:T(8,128)}, f32[2,400,1024]{2,1,0:T(8,128)}) custom-call(f32[8,128]{1,0:T(8,128)} %get-tuple-element.39.refs_0_, f32[2,400,1024]{2,1,0:T(8,128)} %refs_1_.3, f32[2,400,1024]{2,1,0:T(8,128)} %refs_2_.3, bf16[2,400,1024]{2,1,0:T(8,128)(2,1)} %get-tuple-element.55.refs_3_), custom_call_target="tpu_custom_call" | custom-call | flops 29491200 | bytes 14745600 | tf_op jit(solution)/shard_map/finish/pallas_call | solution.py:583
  527.0 0.0 collective-permute-done.1.other_ref
  527.0 3.2 fill.1
Async XLA Ops:
  477.9 40.1 %collective-permute-start = (bf16[2,128,3200]{2,1,0:T(8,128)(2,1)}, bf16[2,128,3200]{2,1,0:T(8,128)(2,1)}, u32[]{:S(2)}, u32[]{:S(2)}) collective-permute-start(bf16[2,128,3200]{2,1,0:T(8,128)(2,1)} %get-tuple-element.38.far_ref), channel_id=1, source_target_pairs={{2,0},{3,1},{4,6},{5,7},{10,8},{11,9},{12,14},{13,15},{18,16},{19,... | collective-permute-start | bytes 4915208 | tf_op jit(solution)/shard_map/ppermute | solution.py:645
  518.1 8.9 %collective-permute-start.1 = (bf16[2,128,3200]{2,1,0:T(8,128)(2,1)}, bf16[2,128,3200]{2,1,0:T(8,128)(2,1)}, u32[]{:S(2)}, u32[]{:S(2)}) collective-permute-start(bf16[2,128,3200]{2,1,0:T(8,128)(2,1)} %collective-permute-done.mine_ref), channel_id=1, source_target_pairs={{0,1},{1,0},{6,7},{7,6},{8,9},{9,8},{14,15},{15,14},{16,17},{17,16... | collective-permute-start | bytes 4915208 | tf_op jit(solution)/shard_map/ppermute | solution.py:649

commit v5 on v4

--- a/solution.py
+++ b/solution.py
@@ -593,47 +593,49 @@
     return got[:nc], got[nc : nc + ns], got[nc + ns :]
 
 
-def fill(whole, far, mine, other):
-    size = far.shape
-
-    def copy(whole_ref, far_ref, mine_ref, other_ref, out_ref, buf, get, put):
+def fill(whole, middle, end, other):
+    size = end.shape
+
+    def copy(whole_ref, middle_ref, end_ref, out_ref, buf, get, put):
         me = lax.axis_index("dp")
         z, core = me // 2, lax.rem(me, 2)
         is_end = (z == 0) | (z == 3)
         block = jnp.where(z < 2, 3, 0)
-
-        def move(sources):
-            first = [(2 * block + cc) * size[1] for cc in (core, 1 - core)]
-            ins = [pltpu.make_async_copy(src, buf.at[i], get.at[i]) for i, src in enumerate(sources)]
+        first = (2 * block + (1 - core if other else core)) * size[1]
+
+        def move(src):
+            ins = [pltpu.make_async_copy(src.at[l], buf.at[l], get.at[l]) for l in range(2)]
+            outs = [pltpu.make_async_copy(buf.at[l], out_ref.at[l, pl.ds(tiled(first), size[1])], put.at[l]) for l in range(2)]
             for one in ins:
                 one.start()
-            outs = []
-            for i, one in enumerate(ins):
-                one.wait()
-                outs.append(pltpu.make_async_copy(buf.at[i], out_ref.at[:, pl.ds(tiled(first[i]), size[1])], put.at[i]))
-                outs[i].start()
+            for l in range(2):
+                ins[l].wait()
+                outs[l].start()
             for one in outs:
                 one.wait()
 
         @pl.when(is_end)
         def _():
-            move((mine_ref, other_ref))
-
-        @pl.when(jnp.logical_not(is_end))
-        def _():
-            move((far_ref,))
+            move(end_ref)
+
+        if not other:
+
+            @pl.when(jnp.logical_not(is_end))
+            def _():
+                move(middle_ref)
 
     any_ = pl.BlockSpec(memory_space=pl.ANY)
     return pl.pallas_call(
         copy,
         name="fill",
-        in_specs=[any_] * 4,
+        in_specs=[any_] * 3,
         out_specs=any_,
         out_shape=jax.ShapeDtypeStruct(whole.shape, whole.dtype),
-        scratch_shapes=[pltpu.VMEM((2, *size), whole.dtype)] + [pltpu.SemaphoreType.DMA((2,))] * 2,
+        scratch_shapes=[pltpu.VMEM(size, whole.dtype)] + [pltpu.SemaphoreType.DMA((2,))] * 2,
         input_output_aliases={0: 0},
         compiler_params=pltpu.CompilerParams(vmem_limit_bytes=ALL_VMEM),
-    )(whole, far, mine, other)
+        cost_estimate=pl.CostEstimate(flops=whole.size, bytes_accessed=whole.size, transcendentals=0),
+    )(whole, middle, end)
 
 
 def solution(mesh):
@@ -644,13 +646,12 @@
 
         mine = lax.ppermute(far, "dp", [(2, 0), (3, 1), (4, 6), (5, 7)])
         sets = list(zip(m, v, gradients, strict=True))
-        whole, new_m, new_v = finish(new, sets[:2], factor)
+        whole, new_m, new_v = finish(new, sets, factor)
         mine, whole, new_m, new_v = lax.optimization_barrier((mine, whole, new_m, new_v))
         other = lax.ppermute(mine, "dp", [(0, 1), (1, 0), (6, 7), (7, 6)])
-        _, last_m, last_v = finish([], sets[2:], factor)
         gate, up, down = whole
-        up, other, last_m, last_v = lax.optimization_barrier((up, other, last_m, last_v))
-        return (gate, fill(up, far, mine, other), down, *new_m, *last_m, *new_v, *last_v)
+        up, other = lax.optimization_barrier((fill(up, far, mine, 0), other))
+        return (gate, fill(up, other, other, 1), down, *new_m, *new_v)
 
     all_of, cut = P(), P(None, "dp")
     return jax.shard_map(

time: 531 us -> 529 us (level)
    pallas_call x2 -> x1, Pallas kernels: 44.8 us -> 41.8 us  [finish(): pl.pallas_call(run, name='finish', in_specs=[pl.BlockSpec(memory_space=pl...]
where the time goes in v5:
time: 529 us
  Pallas kernels  524 us (99%)
    pallas_call x1, Pallas kernels, exchange(): pl.pallas_call(kernel, name='exchange', out_shape=(*whole, *block, *momen...  477 us
    pallas_call x1, Pallas kernels, finish(): pl.pallas_call(run, name='finish', in_specs=[pl.BlockSpec(memory_space=pl...  41.8 us
  transfers between devices with their start and end apart: 2, of which 1 were waited for; matrix products, arithmetic and copies ran while one was open for 0% of the time, Pallas kernels for 8%

profile of v5, /device:TPU:0, one launch (start us, length us, event | category | flops | bytes accessed | tf_op | source)
XLA Modules:
  0.0 528.7 jit_solution(17308990902795539303)
XLA Ops:
  0.6 477.3 %exchange.1 = (bf16[2,1024,3200]{2,1,0:T(8,128)(2,1)}, bf16[2,1024,3200]{2,1,0:T(8,128)(2,1)}, bf16[2,3200,1024]{2,1,0:T(8,128)(2,1)}, bf16[2,128,3200]{2,1,0:T(...) custom-call(bf16[1,2,1024,3200]{3,2,1,0:T(8,128)(2,1)} %refs_0_.1, ...), custom_call_target="tpu_custom_call" | custom-call | tf_op jit(solution)/shard_map/exchange/pallas_call | solution.py:474
  477.9 1.3 collective-permute-start
  479.2 41.8 %finish.1 = (bf16[2,1024,3200]{2,1,0:T(8,128)(2,1)}, bf16[2,1024,3200]{2,1,0:T(8,128)(2,1)}, bf16[2,3200,1024]{2,1,0:T(8,128)(2,1)}, f32[2,128,3200]{2,1,0:T(8,1...) custom-call(f32[8,128]{1,0:T(8,128)} %get-tuple-element.39.refs_0_, ...), custom_call_target="tpu_custom_call" | custom-call | flops 245760000 | bytes 122880000 | tf_op jit(solution)/shard_map/finish/pallas_call | solution.py:583
  521.0 0.0 collective-permute-done.end_ref
  521.0 2.2 collective-permute-start.1
  523.3 2.4 fill.2.whole_ref
  525.6 0.7 collective-permute-done.1.middle_ref.end_ref
  526.4 2.3 fill.3
Async XLA Ops:
  477.9 43.1 %collective-permute-start = (bf16[2,128,3200]{2,1,0:T(8,128)(2,1)}, bf16[2,128,3200]{2,1,0:T(8,128)(2,1)}, u32[]{:S(2)}, u32[]{:S(2)}) collective-permute-start(bf16[2,128,3200]{2,1,0:T(8,128)(2,1)} %get-tuple-element.38.middle_ref), channel_id=1, source_target_pairs={{2,0},{3,1},{4,6},{5,7},{10,8},{11,9},{12,14},{13,15},{18,16},{19,... | collective-permute-start | bytes 4915208 | tf_op jit(solution)/shard_map/ppermute | solution.py:647
  521.0 5.3 %collective-permute-start.1 = (bf16[2,128,3200]{2,1,0:T(8,128)(2,1)}, bf16[2,128,3200]{2,1,0:T(8,128)(2,1)}, u32[]{:S(2)}, u32[]{:S(2)}) collective-permute-start(bf16[2,128,3200]{2,1,0:T(8,128)(2,1)} %collective-permute-done.end_ref), channel_id=1, source_target_pairs={{0,1},{1,0},{6,7},{7,6},{8,9},{9,8},{14,15},{15,14},{16,17},{17,16... | collective-permute-start | bytes 4915208 | tf_op jit(solution)/shard_map/ppermute | solution.py:651
